TPU v7x, 32 devices: a 4x4x1 block of a 4x4x8 slice. The times are simulated.
32 devices in a mesh: dp: 1 (over z), col: 4 (over y), row: 8 (over x, core).
Axes of the slice: x: 4, y: 4, z: 1, core: 2. Of those that a mesh axis runs over, the one named last changes fastest.
The devices are a block of a 4x4x8 slice.
Arguments:
- latent: bfloat16 [4, 16, 384, 640], P('dp', 'row', 'col')
- t_emb: bfloat16 [4, 1280], P('dp')
- res_norm: bfloat16 [2, 2, 2, 640], replicated
- res_conv: bfloat16 [2, 2, 3, 3, 640, 640], replicated
- res_temb: bfloat16 [2, 1280, 640], replicated
- attn_norm: bfloat16 [2, 640], replicated
- attn_proj: bfloat16 [4, 10, 640, 64], replicated
Outputs:
- output: bfloat16 [4, 16, 384, 640], P('dp', 'row', 'col')
All inputs are finite; a program needn't handle non-finite values.
Results may differ from a plain program's by a relative error of at most 0.0114891.
Values are sent between devices in bfloat16 or wider.
A program may use at most 768 MiB of HBM per device.

v0:
```python
import jax
import jax.numpy as jnp
from jax import lax
from jax.sharding import PartitionSpec as P

GROUPS = 32
EPS = 1e-5


def group_norm(values, gn_scale, gn_shift, n_dev):
    n_batch, n_rows, n_cols, n_chan = values.shape
    group_ch = n_chan // GROUPS
    grouped = values.astype(jnp.float32).reshape(n_batch, n_rows, n_cols, GROUPS, group_ch)
    part_sums = jnp.stack([jnp.sum(grouped, axis=(1, 2, 4)), jnp.sum(grouped * grouped, axis=(1, 2, 4))])
    moments = lax.psum(part_sums, ('row', 'col')) / (n_rows * n_cols * group_ch * n_dev)
    mean_val = moments[0]
    inv_std = lax.rsqrt(moments[1] - mean_val * mean_val + EPS)
    normed = (grouped - mean_val[:, None, None, :, None]) * inv_std[:, None, None, :, None]
    return normed.reshape(values.shape) * gn_scale.astype(jnp.float32) + gn_shift.astype(jnp.float32)


def halo_conv(acts_in, kernel, n_row, n_col):
    to_next_row = [(i, i + 1) for i in range(n_row - 1)]
    to_prev_row = [(i + 1, i) for i in range(n_row - 1)]
    to_next_col = [(i, i + 1) for i in range(n_col - 1)]
    to_prev_col = [(i + 1, i) for i in range(n_col - 1)]
    from_above = lax.ppermute(acts_in[:, -1:], 'row', to_next_row)
    from_below = lax.ppermute(acts_in[:, :1], 'row', to_prev_row)
    row_padded = jnp.concatenate([from_above, acts_in, from_below], axis=1)
    from_left = lax.ppermute(row_padded[:, :, -1:], 'col', to_next_col)
    from_right = lax.ppermute(row_padded[:, :, :1], 'col', to_prev_col)
    padded = jnp.concatenate([from_left, row_padded, from_right], axis=2)
    return lax.conv_general_dilated(padded, kernel, (1, 1), 'VALID', dimension_numbers=('NHWC', 'HWIO', 'NHWC'), preferred_element_type=jnp.float32)


def res_block(latent, t_emb, norm_par, kernels, w_temb, n_row, n_col):
    n_dev = n_row * n_col
    t_act = jax.nn.silu(t_emb.astype(jnp.float32)).astype(jnp.bfloat16)
    t_proj = jnp.dot(t_act, w_temb, preferred_element_type=jnp.float32)
    first_act = jax.nn.silu(group_norm(latent, norm_par[0, 0], norm_par[0, 1], n_dev)).astype(jnp.bfloat16)
    hidden = (halo_conv(first_act, kernels[0], n_row, n_col) + t_proj[:, None, None, :]).astype(jnp.bfloat16)
    second_act = jax.nn.silu(group_norm(hidden, norm_par[1, 0], norm_par[1, 1], n_dev)).astype(jnp.bfloat16)
    return (latent.astype(jnp.float32) + halo_conv(second_act, kernels[1], n_row, n_col)).astype(jnp.bfloat16)


def attend(queries, keys_all, values_all, n_blocks):
    n_batch, n_query, n_heads, head_dim = queries.shape
    blk_len = keys_all.shape[1] // n_blocks
    key_blocks = keys_all.reshape(n_batch, n_blocks, blk_len, n_heads, head_dim)
    val_blocks = values_all.reshape(n_batch, n_blocks, blk_len, n_heads, head_dim)
    inv_scale = head_dim ** -0.5

    def key_step(blk_idx, loop_state):
        run_max, run_sum, out_acc = loop_state
        key_blk = lax.dynamic_index_in_dim(key_blocks, blk_idx, axis=1, keepdims=False)
        val_blk = lax.dynamic_index_in_dim(val_blocks, blk_idx, axis=1, keepdims=False)
        logits = jnp.einsum('bqhd,bkhd->bhqk', queries, key_blk, preferred_element_type=jnp.float32) * inv_scale
        new_max = jnp.maximum(run_max, jnp.max(logits, axis=-1))
        rescale = jnp.exp(run_max - new_max)
        exp_logits = jnp.exp(logits - new_max[..., None])
        run_sum = run_sum * rescale + jnp.sum(exp_logits, axis=-1)
        out_acc = out_acc * rescale[..., None] + jnp.einsum('bhqk,bkhd->bhqd', exp_logits.astype(jnp.bfloat16), val_blk, preferred_element_type=jnp.float32)
        return new_max, run_sum, out_acc

    carry_init = (jnp.full((n_batch, n_heads, n_query), -jnp.inf, jnp.float32), jnp.zeros((n_batch, n_heads, n_query), jnp.float32), jnp.zeros((n_batch, n_heads, n_query, head_dim), jnp.float32))
    run_max, run_sum, out_acc = lax.fori_loop(0, n_blocks, key_step, carry_init)
    return out_acc / run_sum[..., None]


def attn_block(latent, norm_par, proj_w, n_dev):
    n_batch, n_rows, n_cols, n_chan = latent.shape
    normed = group_norm(latent, norm_par[0], norm_par[1], n_dev).astype(jnp.bfloat16).reshape(n_batch, n_rows * n_cols, n_chan)
    qkv_loc = jnp.einsum('bnc,khcd->kbnhd', normed, proj_w[:3], preferred_element_type=jnp.float32).astype(jnp.bfloat16)
    kv_all = lax.all_gather(qkv_loc[1:], ('row', 'col'), axis=2, tiled=True)
    attn_out = attend(qkv_loc[0], kv_all[0], kv_all[1], n_dev).astype(jnp.bfloat16)
    out_proj = jnp.einsum('bhqd,hcd->bqc', attn_out, proj_w[3], preferred_element_type=jnp.float32)
    return (latent.astype(jnp.float32) + out_proj.reshape(latent.shape)).astype(jnp.bfloat16)


def solution(mesh):
    n_row = mesh.shape['row']
    n_col = mesh.shape['col']

    def run_stage(latent, t_emb, res_norm, res_conv, res_temb, attn_norm, attn_proj):
        hidden = res_block(latent, t_emb, res_norm[0], res_conv[0], res_temb[0], n_row, n_col)
        hidden = attn_block(hidden, attn_norm, attn_proj, n_row * n_col)
        return res_block(hidden, t_emb, res_norm[1], res_conv[1], res_temb[1], n_row, n_col)

    spec_x = P('dp', 'row', 'col', None)
    return jax.shard_map(run_stage, mesh=mesh, in_specs=(spec_x, P('dp', None), P(), P(), P(), P(), P()), out_specs=spec_x, check_vma=False)
```

profile of v0, /device:TPU:97, one launch (start us, length us, event | category | flops | bytes accessed | tf_op | source)
XLA Modules:
  0.0 1577.5 jit_solution(12235794380705037307)
XLA Ops:
  8.6 49.8 %psum.35 = f32[2,4,32]{2,1,0:T(4,128)S(1)} all-reduce(f32[2,4,32]{2,1,0:T(4,128)S(1)} %pad_maximum_fusion.12), channel_id=1, replica_groups=mesh['dp'=1,'col'=4,'row'=8] {'row','col'}, use_global_device_ids=true, to_apply=%region_4.5 | all-reduce | flops 256 | bytes 2048 | tf_op jit(solution)/shard_map/psum | solution.py:15
  85.7 12.2 fusion.155
  104.0 45.5 %psum.36 = f32[2,4,32]{2,1,0:T(4,128)S(1)} all-reduce(f32[2,4,32]{2,1,0:T(4,128)S(1)} %pad_maximum_fusion.13), channel_id=1, replica_groups=mesh['dp'=1,'col'=4,'row'=8] {'row','col'}, use_global_device_ids=true, to_apply=%region_9.10 | all-reduce | flops 256 | bytes 2048 | tf_op jit(solution)/shard_map/psum | solution.py:15
  182.1 10.8 fusion.87
  196.1 45.4 %psum.37 = f32[2,4,32]{2,1,0:T(4,128)S(1)} all-reduce(f32[2,4,32]{2,1,0:T(4,128)S(1)} %pad_maximum_fusion.14), channel_id=1, replica_groups=mesh['dp'=1,'col'=4,'row'=8] {'row','col'}, use_global_device_ids=true, to_apply=%region_14.15 | all-reduce | flops 256 | bytes 2048 | tf_op jit(solution)/shard_map/psum | solution.py:15
  256.3 345.6 %all-gather.2.cloned.1.call-done = bf16[2,4,6144,10,64]{4,1,3,0,2:T(4,128)(2,1)} async-done(((bf16[2,4,192,10,64]{4,1,3,0,2:T(4,128)(2,1)}), bf16[2,4,6144,10,64]{4,1,3,0,2:T(4,128)(2,1)}) %all-gather.2.cloned.1.call-update) | async-done | bytes 62914576 | tf_op jit(solution)/shard_map/all_gather | solution.py:74
  601.8 83.7 %fusion.150 = (bf16[1,4,6144,10,64]{4,1,3,0,2:T(4,128)(2,1)}, bf16[1,4,6144,10,64]{4,1,3,0,2:T(4,128)(2,1)}) fusion(bf16[2,4,6144,10,64]{4,1,3,0,2:T(4,128)(2,1)} %all-gather.2.cloned.1.call-done), kind=kLoop, calls=%fused_computation.212 | loop fusion | bytes 125829120 | tf_op jit(solution)/shard_map/slice | solution.py:75
  685.6 85.1 %copy.104 = bf16[4,32,192,10,64]{2,4,3,0,1:T(8,128)(2,1)} copy(bf16[4,32,192,10,64]{4,0,3,2,1:T(4,128)(2,1)} %bitcast.254) | data formatting | bytes 62914560
  770.6 85.1 %copy.105 = bf16[4,32,192,10,64]{2,4,3,0,1:T(8,128)(2,1)} copy(bf16[4,32,192,10,64]{4,0,3,2,1:T(4,128)(2,1)} %bitcast.253) | data formatting | bytes 62914560
  855.7 528.3 %while.18 = (s32[]{:T(128)}, f32[4,10,192]{2,1,0:T(8,128)S(1)}, f32[4,10,192]{2,1,0:T(8,128)S(1)}, f32[4,10,192,64]{2,3,1,0:T(8,128)}, bf16[4,32,192,10,64]{2,4,...) while((s32[]{:T(128)}, f32[4,10,192]{2,1,0:T(8,128)S(1)}, ...), condition=%wide.region_18.19_spmd.clone, body=%wide.region_15.18_spmd.clone.sunk | while | flops 390796800 | bytes 49972356 | solution.py:66
  855.7 5.7 bitcast_reduce_fusion.2
  871.4 5.7 bitcast_reduce_fusion.2
  887.9 5.7 bitcast_reduce_fusion.2
  899.1 5.4 fusion.170
  904.5 5.7 bitcast_reduce_fusion.2
  915.6 5.4 fusion.170
  921.0 5.7 bitcast_reduce_fusion.2
  937.5 5.7 bitcast_reduce_fusion.2
  948.7 5.4 fusion.170
  954.1 5.7 bitcast_reduce_fusion.2
  965.2 5.4 fusion.170
  970.6 5.7 bitcast_reduce_fusion.2
  987.1 5.7 bitcast_reduce_fusion.2
  998.3 5.4 fusion.170
  1003.7 5.7 bitcast_reduce_fusion.2
  1014.8 5.4 fusion.170
  1020.2 5.7 bitcast_reduce_fusion.2
  1036.8 5.7 bitcast_reduce_fusion.2
  1047.9 5.4 fusion.170
  1053.3 5.7 bitcast_reduce_fusion.2
  1064.4 5.4 fusion.170
  1069.8 5.7 bitcast_reduce_fusion.2
  1086.4 5.7 bitcast_reduce_fusion.2
  1097.5 5.4 fusion.170
  1102.9 5.7 bitcast_reduce_fusion.2
  1114.1 5.4 fusion.170
  1119.4 5.7 bitcast_reduce_fusion.2
  1136.0 5.7 bitcast_reduce_fusion.2
  1147.1 5.4 fusion.170
  1152.5 5.7 bitcast_reduce_fusion.2
  1163.7 5.4 fusion.170
  1169.0 5.7 bitcast_reduce_fusion.2
  1185.6 5.7 bitcast_reduce_fusion.2
  1196.7 5.4 fusion.170
  1202.1 5.7 bitcast_reduce_fusion.2
  1213.3 5.4 fusion.170
  1218.7 5.7 bitcast_reduce_fusion.2
  1235.2 5.7 bitcast_reduce_fusion.2
  1246.3 5.4 fusion.170
  1251.7 5.7 bitcast_reduce_fusion.2
  1262.9 5.4 fusion.170
  1268.3 5.7 bitcast_reduce_fusion.2
  1284.8 5.7 bitcast_reduce_fusion.2
  1301.3 5.7 bitcast_reduce_fusion.2
  1312.5 5.4 fusion.170
  1317.9 5.7 bitcast_reduce_fusion.2
  1334.4 5.7 bitcast_reduce_fusion.2
  1350.9 5.7 bitcast_reduce_fusion.2
  1362.1 5.4 fusion.170
  1367.5 5.7 bitcast_reduce_fusion.2
  1390.9 44.9 %psum.38 = f32[2,4,32]{2,1,0:T(4,128)S(1)} all-reduce(f32[2,4,32]{2,1,0:T(4,128)S(1)} %pad_maximum_fusion.15), channel_id=1, replica_groups=mesh['dp'=1,'col'=4,'row'=8] {'row','col'}, use_global_device_ids=true, to_apply=%region_23.24 | all-reduce | flops 256 | bytes 2048 | tf_op jit(solution)/shard_map/psum | solution.py:15
  1462.2 12.2 fusion.156
  1480.5 45.2 %psum.39 = f32[2,4,32]{2,1,0:T(4,128)S(1)} all-reduce(f32[2,4,32]{2,1,0:T(4,128)S(1)} %pad_maximum_fusion.16), channel_id=1, replica_groups=mesh['dp'=1,'col'=4,'row'=8] {'row','col'}, use_global_device_ids=true, to_apply=%region_28.29 | all-reduce | flops 256 | bytes 2048 | tf_op jit(solution)/shard_map/psum | solution.py:15
  1555.3 10.8 fusion.96
  (427 shorter events, 407.4 us)
Async XLA Ops:
  6.5 53.6 %copy-start.1 = (bf16[4,2,96,640]{3,2,1,0:T(8,128)(2,1)S(1)}, bf16[4,2,96,640]{3,2,1,0:T(8,128)(2,1)}, u32[]{:S(2)}) copy-start(bf16[4,2,96,640]{3,2,1,0:T(8,128)(2,1)} %param.9) | copy-start | bytes 2949124
  6.5 595.3 %all-gather.2.cloned.1.call-start = ((), (), s32[]{:S(2)}) async-start(), calls=%async_computation | async-start | bytes 129761280 | tf_op jit(solution)/shard_map/all_gather | solution.py:74
  60.9 16.3 %copy-start.14 = (bf16[2,1280,640]{2,1,0:T(8,128)(2,1)S(1)}, bf16[2,1280,640]{2,1,0:T(8,128)(2,1)}, u32[]{:S(2)}) copy-start(bf16[2,1280,640]{2,1,0:T(8,128)(2,1)} %param.13) | copy-start | bytes 9830404
  60.9 16.3 %copy-start.16 = (bf16[4,1280]{1,0:T(4,128)(2,1)S(1)}, bf16[4,1280]{1,0:T(4,128)(2,1)}, u32[]{:S(2)}) copy-start(bf16[4,1280]{1,0:T(4,128)(2,1)} %param.10) | copy-start | bytes 30724
  61.0 8.0 collective-permute-start
  63.2 10.2 collective-permute-start.1
  73.5 4.1 collective-permute-start.2
  75.9 4.8 collective-permute-start.3
  97.9 1.7 copy-start.2
  149.9 1.6 copy-start.3
  155.4 7.9 collective-permute-start.4
  158.0 10.2 collective-permute-start.5
  165.1 7.4 copy-start.13
  169.0 3.5 collective-permute-start.6
  171.2 4.6 collective-permute-start.7
  195.7 46.7 %copy-start.5 = (bf16[4,2,96,640]{3,2,1,0:T(8,128)(2,1)}, bf16[4,2,96,640]{3,2,1,0:T(8,128)(2,1)S(1)}, u32[]{:S(2)}) copy-start(bf16[4,2,96,640]{3,2,1,0:T(8,128)(2,1)S(1)} %get-tuple-element.216) | copy-start | bytes 2949124
  247.5 1.9 copy-start.4
  861.4 5.5 copy-start
  877.1 5.5 copy-start
  893.6 5.5 copy-start
  910.2 5.5 copy-start
  926.7 5.5 copy-start
  943.2 5.5 copy-start
  959.8 5.5 copy-start
  976.3 5.5 copy-start
  992.8 5.5 copy-start
  1009.4 5.5 copy-start
  1025.9 5.5 copy-start
  1042.4 5.5 copy-start
  1059.0 5.5 copy-start
  1075.5 5.5 copy-start
  1092.0 5.5 copy-start
  1108.6 5.5 copy-start
  1125.1 5.5 copy-start
  1141.7 5.5 copy-start
  1158.2 5.5 copy-start
  1174.7 5.5 copy-start
  1191.3 5.5 copy-start
  1207.8 5.5 copy-start
  1224.3 5.5 copy-start
  1240.9 5.5 copy-start
  1257.4 5.5 copy-start
  1273.9 5.5 copy-start
  1290.5 5.5 copy-start
  1307.0 5.5 copy-start
  1323.6 5.5 copy-start
  1340.1 5.5 copy-start
  1356.6 5.5 copy-start
  1373.2 5.5 copy-start
  1386.1 1.6 copy-start.6
  1387.7 48.6 %copy-start.11 = (f32[640]{0:T(1024)S(1)}, f32[640]{0:T(1024)}, u32[]{:S(2)}) copy-start(f32[640]{0:T(1024)} %get-tuple-element.192) | copy-start | bytes 7684
  1387.7 48.6 %copy-start.12 = (f32[640]{0:T(1024)S(1)}, f32[640]{0:T(1024)}, u32[]{:S(2)}) copy-start(f32[640]{0:T(1024)} %get-tuple-element.193) | copy-start | bytes 7684
  1390.5 46.6 %copy-start.7 = (bf16[4,2,96,640]{3,2,1,0:T(8,128)(2,1)}, bf16[4,2,96,640]{3,2,1,0:T(8,128)(2,1)S(1)}, u32[]{:S(2)}) copy-start(bf16[4,2,96,640]{3,2,1,0:T(8,128)(2,1)S(1)} %get-tuple-element.241) | copy-start | bytes 2949124
  1437.0 16.7 %copy-start.15 = (bf16[2,1280,640]{2,1,0:T(8,128)(2,1)S(1)}, bf16[2,1280,640]{2,1,0:T(8,128)(2,1)}, u32[]{:S(2)}) copy-start(bf16[2,1280,640]{2,1,0:T(8,128)(2,1)} %param.13) | copy-start | bytes 9830404
  1437.0 16.7 %copy-start.17 = (bf16[4,1280]{1,0:T(4,128)(2,1)S(1)}, bf16[4,1280]{1,0:T(4,128)(2,1)}, u32[]{:S(2)}) copy-start(bf16[4,1280]{1,0:T(4,128)(2,1)} %param.10) | copy-start | bytes 30724
  1437.1 9.4 collective-permute-start.8
  1440.8 10.2 collective-permute-start.9
  1451.0 3.0 collective-permute-start.10
  1452.4 5.0 collective-permute-start.11
  1528.5 7.7 collective-permute-start.12
  1530.9 10.2 collective-permute-start.13
  1541.9 3.7 collective-permute-start.14
  1544.3 4.6 collective-permute-start.15
  1567.8 1.2 copy-start.8
  (4 other events, 3.6 us)
Sparse Core Ops, SparseCore 0:
  254.9 346.8 all-gather.1
where the time goes:
time: 1590 us; the launch traced here: 1580 us
  matrix products  407 us (26%)
  waiting for transfers between devices  384 us (24%)
  local copies, waits for them, and re-layouts  316 us (20%)
  blocking collectives  231 us (15%)
  other arithmetic  191 us (12%)
  starting transfers between devices  33.5 us (2%)
    all_gather x1, waiting for transfers between devices, attn_block(): kv_all = lax.all_gather(qkv_loc[1:], ('row', 'col'), axis=2, tiled=True)  346 us
    psum x5, blocking collectives, group_norm(): lax.psum(part_sums, ('row', 'col')) / (n_rows * n_cols * group_ch * n_dev)  231 us
    dot_general x32, matrix products, key_step(): jnp.einsum('bqhd,bkhd->bhqk', queries, key_blk, preferred_element_type=jn...  181 us
    unnamed x44, local copies, waits for them, and re-layouts  177 us
    dot_general x32, matrix products, key_step(): jnp.einsum('bhqk,bkhd->bhqd', exp_logits.astype(jnp.bfloat16), val_blk, p...  171 us
    reduce_sum x32, other arithmetic, key_step(): run_sum = run_sum * rescale + jnp.sum(exp_logits, axis=-1)  163 us
    slice x1, local copies, waits for them, and re-layouts, attn_block(): kv_all[1]  83.7 us
    conv_general_dilated x4, matrix products, halo_conv(): lax.conv_general_dilated(padded, kernel, (1, 1), 'VALID', dimension_numbe...  46 us
  transfers between devices with their start and end apart: 17, of which 13 were waited for; matrix products, arithmetic and copies ran while one was open for 1% of the time, Pallas kernels for 0%

commit v1 on v0

v1 whole, which is shorter than its diff:
```python
import functools

import jax
import jax.numpy as jnp
import numpy as np
from jax import lax
from jax.experimental import pallas as pl
from jax.experimental.pallas import tpu as pltpu
from jax.sharding import PartitionSpec as P

GROUPS = 32
EPS = 1e-5
F32 = jnp.float32
BF16 = jnp.bfloat16
LOG2E = 1.4426950408889634
KEY_BLK = 512


class Place:
    def __init__(self, dims):
        self.n_img, self.n_row, self.n_col, self.rows, self.cols, self.chan = dims
        self.halves = self.n_row // self.n_img
        self.seg = self.n_row // self.halves
        self.row = lax.axis_index('row')
        self.col = lax.axis_index('col')
        self.img = self.row // self.halves
        self.half = self.row % self.halves
        self.n_peer = self.halves * self.n_col
        self.me = self.half * self.n_col + self.col

    def peer(self, step):
        slot = (self.me + step) % self.n_peer
        return {'row': self.img * self.halves + slot // self.n_col, 'col': slot % self.n_col}

    def partner(self):
        return {'row': self.img * self.halves + (1 - self.half), 'col': self.col}

    def beside(self, step, other=False):
        half = (1 - self.half) if other else self.half
        return {'row': self.img * self.halves + half, 'col': (self.col + step + self.n_col) % self.n_col}


def remote(src, dst, send_sem, recv_sem, device):
    return pltpu.make_async_remote_copy(src_ref=src, dst_ref=dst, send_sem=send_sem, recv_sem=recv_sem, device_id=device, device_id_type=pl.DeviceIdType.MESH)


def signal_peers(at, with_column):
    barrier = pltpu.get_barrier_semaphore()
    for step in range(1, at.n_peer):
        pl.semaphore_signal(barrier, inc=1, device_id=at.peer(step), device_id_type=pl.DeviceIdType.MESH)
    count = at.n_peer - 1
    if with_column:
        for step in range(1, at.n_img):
            for half in range(at.halves):
                row = ((at.img + step) % at.n_img) * at.halves + half
                pl.semaphore_signal(barrier, inc=1, device_id={'row': row, 'col': at.col}, device_id_type=pl.DeviceIdType.MESH)
                count += 1
    return count


def wait_peers(count):
    pl.semaphore_wait(pltpu.get_barrier_semaphore(), count)


def stat_copies(at, mine, every, ssem, rsem):
    out = []
    for step in range(1, at.n_peer):
        send = remote(mine, every.at[at.me], ssem.at[step - 1], rsem.at[step - 1], at.peer(step))
        source = (at.me - step + at.n_peer) % at.n_peer
        recv = remote(mine, every.at[source], ssem.at[step - 1], rsem.at[step - 1], at.peer(step))
        out.append((send, recv))
    return out


def halo_copies(at, full, hrow, colbuf, hcol, ssem, rsem):
    base = at.n_peer - 1
    edge = (at.rows * at.seg - 1) * (1 - at.half)
    out = []
    copy = remote(full.at[edge], hrow, ssem.at[base], rsem.at[base], at.partner())
    out.append((copy, copy))
    for slot, (side, step, other) in enumerate([(1, 1, False), (1, 1, True), (0, -1, False), (0, -1, True)]):
        copy = remote(colbuf.at[side], hcol.at[slot], ssem.at[base + 1 + slot], rsem.at[base + 1 + slot], at.beside(step, other))
        out.append((copy, copy))
    return out


def put_stats(stats, mine, every, at):
    s1 = jnp.sum(stats[0], axis=0, keepdims=True)
    s2 = jnp.sum(stats[1], axis=0, keepdims=True)
    idx = lax.broadcasted_iota(jnp.int32, mine.shape, 0)
    both = jnp.where(idx == 0, s1, jnp.where(idx == 1, s2, 0.0))
    mine[...] = both
    every[at.me] = both


def swap_all(at, mine, every, ssem, rsem, full=None, hrow=None, colbuf=None, hcol=None):
    copies = [] if full is None else halo_copies(at, full, hrow, colbuf, hcol, ssem, rsem)
    copies += stat_copies(at, mine, every, ssem, rsem)
    for send, _ in copies:
        send.start()
    for _, recv in copies:
        recv.wait_recv()
    for send, _ in copies:
        send.wait_send()


def norm_terms(every, member, scale, shift, count):
    total = every[0]
    for slot in range(1, every.shape[0]):
        total = total + every[slot]
    high = total.astype(BF16).astype(F32)
    mid = (total - high).astype(BF16).astype(F32)
    low = (total - high - mid).astype(BF16).astype(F32)
    stacked = jnp.concatenate([high, mid, low, jnp.zeros_like(low)], axis=0).astype(BF16)
    n = total.shape[0]
    summed = jnp.dot(stacked, member[...], preferred_element_type=F32)
    sums = summed[0:n] + summed[n:2 * n] + summed[2 * n:3 * n]
    mean = sums[0:1] / count
    var = sums[1:2] / count - mean * mean
    return mean, lax.rsqrt(var + EPS) * scale, shift


def activate(x, terms):
    mean, scale, shift = terms
    u = (x - mean) * scale + shift
    return u / (1.0 + jnp.exp(-u))


def add_stats(stats, vals):
    n, chan = vals.shape
    split = vals.reshape(n // 8, 8, chan)
    return stats[0] + jnp.sum(split, axis=0), stats[1] + jnp.sum(split * split, axis=0)


def zero_stats(chan):
    return jnp.zeros((8, chan), F32), jnp.zeros((8, chan), F32)


def keep_cols(colbuf, first_row, vals, n_rows, cols):
    for k in range(n_rows):
        colbuf[0, pl.ds(first_row + k, 1), :] = vals[k * cols:k * cols + 1]
        colbuf[1, pl.ds(first_row + k, 1), :] = vals[(k + 1) * cols - 1:(k + 1) * cols]


def fill_taps(at, full, hrow, hcol, terms, taps, colact):
    chan, cols = at.chan, at.cols
    n_own = at.rows * at.seg
    for slot in range(4):
        inside = (at.col > 0) if slot < 2 else (at.col < at.n_col - 1)
        colact[slot] = jnp.where(inside, activate(hcol[slot], terms), 0.0)
    row_id = lax.broadcasted_iota(jnp.int32, (cols, chan), 0)

    def put(dst, x, left, right):
        act = activate(x.astype(F32), terms)
        prev = jnp.where(row_id == 0, left, pltpu.roll(act, 1, 0))
        nxt = jnp.where(row_id == cols - 1, right, pltpu.roll(act, cols - 1, 0))
        taps[dst, :, 0:chan] = prev.astype(BF16)
        taps[dst, :, chan:2 * chan] = act.astype(BF16)
        taps[dst, :, 2 * chan:3 * chan] = nxt.astype(BF16)

    def own(r, _):
        put(r + 1, full[r], colact[0, pl.ds(r, 1), :], colact[2, pl.ds(r, 1), :])
        return 0

    lax.fori_loop(0, n_own, own, 0)
    near = (n_own - 1) * at.half
    put((n_own + 1) * (1 - at.half), hrow[...], colact[1, pl.ds(near, 1), :], colact[3, pl.ds(near, 1), :])
    taps[(n_own + 1) * at.half] = jnp.zeros((cols, 3 * chan), BF16)


def conv_rows(at, taps, weights, first):
    acc = None
    for dy in range(3):
        lhs = taps[pl.ds(first + dy, at.rows)].reshape(at.rows * at.cols, 3 * at.chan)
        part = jnp.dot(lhs, weights[dy].reshape(3 * at.chan, at.chan), preferred_element_type=F32)
        acc = part if acc is None else acc + part
    return acc


def norm_rows(ref):
    vals = ref[...].astype(F32)
    return vals[0:1], vals[1:2]


def res_first(dims, count, blk, latent, temb, norms, w_all, member, x_out, stat_out, xin, hid, taps, wbuf, mine, every, hrow, colbuf, hcol, colact, wsem, ssem, rsem, xs, xr, lsem):
    at = Place(dims)
    n_wait = signal_peers(at, True)
    loads = [pltpu.make_async_copy(w_all.at[blk, j], wbuf.at[j], wsem.at[j]) for j in range(2)]
    for load in loads:
        load.start()
    wait_peers(n_wait)
    target_half, slot = at.row // at.seg, at.row % at.seg
    rows, cols, chan = at.rows, at.cols, at.chan
    for i in range(at.n_img):
        row = i * at.halves + target_half
        dst = xin.at[pl.ds(slot * rows, rows)]

        @pl.when(row == at.row)
        def _():
            pltpu.make_async_copy(latent.at[i], dst, lsem).start()

        @pl.when(row != at.row)
        def _():
            remote(latent.at[i], dst, xs.at[i], xr.at[slot], {'row': row, 'col': at.col}).start()

    stats = zero_stats(chan)
    for k in range(at.seg):
        row = at.half * at.seg + k
        dst = xin.at[pl.ds(k * rows, rows)]

        @pl.when(row == at.row)
        def _():
            pltpu.make_async_copy(latent.at[0], dst, lsem).wait()

        @pl.when(row != at.row)
        def _():
            remote(latent.at[0], dst, xs.at[0], xr.at[k], {'row': row, 'col': at.col}).wait_recv()

        vals = xin[k * rows:(k + 1) * rows].astype(F32).reshape(rows * cols, chan)
        stats = add_stats(stats, vals)
        keep_cols(colbuf.at[0], k * rows, vals, rows, cols)
    put_stats(stats, mine.at[0], every.at[0], at)
    swap_all(at, mine.at[0], every.at[0], ssem.at[0], rsem.at[0], xin, hrow.at[0], colbuf.at[0], hcol.at[0])
    for i in range(at.n_img):
        row = i * at.halves + target_half

        @pl.when(row != at.row)
        def _():
            remote(latent.at[i], xin.at[pl.ds(slot * rows, rows)], xs.at[i], xr.at[slot], {'row': row, 'col': at.col}).wait_send()

    conv_pair(at, count, blk, temb, norms, member, xin, hid, taps, wbuf, mine, every, hrow, colbuf, hcol, colact, loads, ssem, rsem)

    def second(m, stats):
        acc = conv_rows(at, taps, wbuf.at[1], m * rows)
        y = (xin[pl.ds(m * rows, rows)].astype(F32).reshape(rows * cols, chan) + acc).astype(BF16)
        x_out[pl.ds(m * rows, rows)] = y.reshape(rows, cols, chan)
        return add_stats(stats, y.astype(F32))

    stats = lax.fori_loop(0, at.seg, second, zero_stats(chan))
    put_stats(stats, mine.at[2], every.at[2], at)
    swap_all(at, mine.at[2], every.at[2], ssem.at[2], rsem.at[2])
    stat_out[...] = every[2]


def conv_pair(at, count, blk, temb, norms, member, xin, hid, taps, wbuf, mine, every, hrow, colbuf, hcol, colact, loads, ssem, rsem):
    rows, cols, chan = at.rows, at.cols, at.chan
    terms = norm_terms(every.at[0], member, *norm_rows(norms.at[blk, 0]), count)
    fill_taps(at, xin, hrow.at[0], hcol.at[0], terms, taps, colact)
    loads[0].wait()
    shift = temb[blk, pl.ds(at.img, 1), :]

    def first(m, stats):
        h = (conv_rows(at, taps, wbuf.at[0], m * rows) + shift).astype(BF16)
        hid[pl.ds(m * rows, rows)] = h.reshape(rows, cols, chan)
        vals = h.astype(F32)
        keep_cols(colbuf.at[1], m * rows, vals, rows, cols)
        return add_stats(stats, vals)

    stats = lax.fori_loop(0, at.seg, first, zero_stats(chan))
    put_stats(stats, mine.at[1], every.at[1], at)
    swap_all(at, mine.at[1], every.at[1], ssem.at[1], rsem.at[1], hid, hrow.at[1], colbuf.at[1], hcol.at[1])
    terms = norm_terms(every.at[1], member, *norm_rows(norms.at[blk, 1]), count)
    fill_taps(at, hid, hrow.at[1], hcol.at[1], terms, taps, colact)
    loads[1].wait()


def nt(a, b):
    return lax.dot_general(a, b, (((1,), (1,)), ((), ())), preferred_element_type=F32)


def attention(dims, count, x, every, norms, proj, member, out, xall, qm, kbuf, vbuf, sbuf, run_max, run_sum, run_out, ssem, rsem, lsem):
    at = Place(dims)
    n_wait = signal_peers(at, False)
    tok, chan = x.shape
    n_head = qm.shape[0]
    dim = chan // n_head
    half_tok = tok // 2
    own_copy = pltpu.make_async_copy(x, xall.at[0], lsem)
    own_copy.start()
    terms = norm_terms(every, member, *norm_rows(norms), count)

    def normed(vals):
        return ((vals.astype(F32) - terms[0]) * terms[1] + terms[2]).astype(BF16)

    right, left, mate = at.beside(1), at.beside(-1), at.partner()
    low, high = pl.ds(0, half_tok), pl.ds(half_tok, half_tok)

    def link(k, src, slot, device):
        return remote(src, slot, ssem.at[k], rsem.at[k], device)

    to_mate = link(0, x, xall.at[1], mate)
    to_right = link(1, x, xall.at[2], right)
    to_left = link(2, x, xall.at[3], left)
    left_mate = link(3, xall.at[2], xall.at[4], mate)
    right_mate = link(4, xall.at[3], xall.at[5], mate)
    left_right = link(5, xall.at[2, low], xall.at[6, low], right)
    right_left = link(6, xall.at[3, high], xall.at[6, high], left)
    far_low = link(7, xall.at[6, low], xall.at[7, low], mate)
    far_high = link(8, xall.at[6, high], xall.at[7, high], mate)
    wait_peers(n_wait)
    to_right.start()
    to_left.start()
    to_mate.start()

    g = normed(x[...])
    qt = nt(proj[0], g).astype(BF16)
    zero = jnp.zeros((dim, tok), BF16)
    for h in range(n_head):
        mine = (h % 2) * dim
        qm[h, mine:mine + dim, :] = qt[h * dim:(h + 1) * dim]
        qm[h, dim - mine:2 * dim - mine, :] = zero
    run_max[...] = jnp.full(run_max.shape, -1e30, F32)
    run_sum[...] = jnp.zeros(run_sum.shape, F32)
    run_out[...] = jnp.zeros(run_out.shape, F32)
    own_copy.wait()

    factor = LOG2E * dim ** -0.5
    n_blk = 2 * tok // KEY_BLK

    def scores(h, j):
        keys = kbuf[pl.ds(j * KEY_BLK, KEY_BLK), pl.ds(pl.multiple_of((h // 2) * 2 * dim, 2 * dim), 2 * dim)]
        return jnp.dot(keys, qm[h], preferred_element_type=F32)

    def phase(k):
        def project(b, _):
            g = normed(xall[2 * k + b])
            span = pl.ds(pl.multiple_of(b * tok, tok), tok)
            kbuf[span, :] = nt(g, proj[1]).astype(BF16)
            vbuf[:, span] = nt(proj[2], g).astype(BF16)
            return 0

        lax.fori_loop(0, 2, project, 0)
        sbuf[0] = scores(0, 0)

        def pair(p, _):
            for u in range(2 * n_blk):
                h, j = 2 * p + u // n_blk, u % n_blk
                if u + 1 < 2 * n_blk:
                    sbuf[(u + 1) % 2] = scores(2 * p + (u + 1) // n_blk, (u + 1) % n_blk)
                else:
                    sbuf[(u + 1) % 2] = scores(jnp.minimum(2 * p + 2, n_head - 1), 0)
                if j == 0:
                    m, l, acc = run_max[h, 0:1], run_sum[h, 0:1], run_out[h]
                s = sbuf[u % 2]
                new = jnp.maximum(m, jnp.max(s, axis=0, keepdims=True) * factor)
                alpha = jnp.exp2(m - new)
                w = jnp.exp2(s * factor - new)
                l = l * alpha + jnp.sum(w, axis=0, keepdims=True)
                vt = vbuf[pl.ds(pl.multiple_of(h * dim, dim), dim), j * KEY_BLK:(j + 1) * KEY_BLK]
                acc = acc * alpha + jnp.dot(vt, w.astype(BF16), preferred_element_type=F32)
                m = new
                if j == n_blk - 1:
                    run_max[h, 0:1], run_sum[h, 0:1], run_out[h] = m, l, acc
            return 0

        lax.fori_loop(0, n_head // 2, pair, 0)

    def at_phase(k, _):
        @pl.when(k == 0)
        def _():
            to_mate.wait_recv()

        @pl.when(k == 1)
        def _():
            to_right.wait_recv()
            left_right.start()
            left_mate.start()
            to_left.wait_recv()
            right_left.start()
            right_mate.start()

        @pl.when(k == 2)
        def _():
            left_mate.wait_recv()
            right_mate.wait_recv()
            left_right.wait_recv()
            far_low.start()
            right_left.wait_recv()
            far_high.start()

        @pl.when(k == 3)
        def _():
            far_low.wait_recv()
            far_high.wait_recv()

        phase(k)
        return 0

    lax.fori_loop(0, 4, at_phase, 0)
    for copy in (to_mate, to_right, to_left, left_mate, right_mate, left_right, right_left, far_low, far_high):
        copy.wait_send()

    def finish(h, _):
        out[pl.ds(pl.multiple_of(h * dim, dim), dim), :] = (run_out[h] / run_sum[h, 0:1]).astype(BF16)
        return 0

    lax.fori_loop(0, n_head, finish, 0)


def res_second(dims, count, blk, x, ot, proj, temb, norms, w_all, member, y_out, xin, hid, taps, wbuf, mine, every, hrow, colbuf, hcol, colact, ybuf, wsem, ssem, rsem, xs, xr, lsem):
    at = Place(dims)
    n_wait = signal_peers(at, True)
    loads = [pltpu.make_async_copy(w_all.at[blk, j], wbuf.at[j], wsem.at[j]) for j in range(2)]
    for load in loads:
        load.start()
    rows, cols, chan = at.rows, at.cols, at.chan
    tile = rows * cols
    add = lax.dot_general(ot[...], proj[...], (((0,), (0,)), ((), ())), preferred_element_type=F32)
    stats = zero_stats(chan)
    for m in range(at.seg):
        y = (x[m * rows:(m + 1) * rows].astype(F32).reshape(tile, chan) + add[m * tile:(m + 1) * tile]).astype(BF16)
        xin[m * rows:(m + 1) * rows] = y.reshape(rows, cols, chan)
        vals = y.astype(F32)
        stats = add_stats(stats, vals)
        keep_cols(colbuf.at[0], m * rows, vals, rows, cols)
    put_stats(stats, mine.at[0], every.at[0], at)
    wait_peers(n_wait)
    swap_all(at, mine.at[0], every.at[0], ssem.at[0], rsem.at[0], xin, hrow.at[0], colbuf.at[0], hcol.at[0])
    conv_pair(at, count, blk, temb, norms, member, xin, hid, taps, wbuf, mine, every, hrow, colbuf, hcol, colact, loads, ssem, rsem)

    def back(m):
        row = at.half * at.seg + m
        src = ybuf.at[pl.ds(m * rows, rows)]
        return row, pltpu.make_async_copy(src, y_out.at[at.img], lsem), remote(src, y_out.at[at.img], xs.at[m], xr.at[at.img], {'row': row, 'col': at.col})

    def second(m, _):
        acc = conv_rows(at, taps, wbuf.at[1], m * rows)
        y = (xin[pl.ds(m * rows, rows)].astype(F32).reshape(tile, chan) + acc).astype(BF16)
        ybuf[pl.ds(m * rows, rows)] = y.reshape(rows, cols, chan)
        row, local, far = back(m)

        @pl.when(row == at.row)
        def _():
            local.start()

        @pl.when(row != at.row)
        def _():
            far.start()

        return 0

    lax.fori_loop(0, at.seg, second, 0)
    for m in range(at.seg):
        row, local, far = back(m)

        @pl.when(row == at.row)
        def _():
            local.wait()

        @pl.when(row != at.row)
        def _():
            far.wait_send()

    for i in range(at.n_img):
        row = i * at.halves + at.row // at.seg

        @pl.when(row != at.row)
        def _():
            remote(ybuf.at[pl.ds(0, rows)], y_out.at[i], xs.at[0], xr.at[i], {'row': row, 'col': at.col}).wait_recv()


def solution(mesh):
    n_row = mesh.shape['row']
    n_col = mesh.shape['col']

    def run_stage(latent, t_emb, res_norm, res_conv, res_temb, attn_norm, attn_proj):
        n_img, rows, cols, chan = latent.shape
        n_head, dim = attn_proj.shape[1], attn_proj.shape[3]
        dims = (n_img, n_row, n_col, rows, cols, chan)
        halves, seg = n_row // n_img, n_row // (n_row // n_img)
        n_peer = halves * n_col
        own = rows * seg
        tok = own * cols
        per_group = chan // GROUPS
        count = float(n_row * rows * n_col * cols * per_group)
        group_id = np.arange(chan) // per_group
        member = jnp.asarray((group_id[:, None] == group_id[None, :]).astype(np.float32), BF16)
        t_act = jax.nn.silu(t_emb.astype(F32)).astype(BF16)
        temb = jnp.einsum('bk,rkc->rbc', t_act, res_temb, preferred_element_type=F32)
        proj = attn_proj.transpose(0, 1, 3, 2).reshape(4, n_head * dim, chan)

        vmem, anywhere = pl.BlockSpec(memory_space=pltpu.VMEM), pl.BlockSpec(memory_space=pl.ANY)
        block = jax.ShapeDtypeStruct((own, cols, chan), BF16)

        def conv_scratch(n_stage):
            n_msg = n_peer - 1 + 5
            return [
                pltpu.VMEM((own, cols, chan), BF16),
                pltpu.VMEM((own, cols, chan), BF16),
                pltpu.VMEM((own + 2, cols, 3 * chan), BF16),
                pltpu.VMEM((2, 3, 3, chan, chan), BF16),
                pltpu.VMEM((n_stage, 8, chan), F32),
                pltpu.VMEM((n_stage, n_peer, 8, chan), F32),
                pltpu.VMEM((2, cols, chan), BF16),
                pltpu.VMEM((2, 2, own, chan), F32),
                pltpu.VMEM((2, 4, own, chan), F32),
                pltpu.VMEM((4, own, chan), F32),
            ], [
                pltpu.SemaphoreType.DMA((2,)),
                pltpu.SemaphoreType.DMA((n_stage, n_msg)),
                pltpu.SemaphoreType.DMA((n_stage, n_msg)),
                pltpu.SemaphoreType.DMA((max(n_img, seg),)),
                pltpu.SemaphoreType.DMA((max(n_img, seg),)),
                pltpu.SemaphoreType.DMA,
            ]

        def params(cid):
            return pltpu.CompilerParams(collective_id=cid, has_side_effects=True, vmem_limit_bytes=60 << 20)

        bufs, sems = conv_scratch(3)
        x1, every = pl.pallas_call(
            functools.partial(res_first, dims, count, 0),
            out_shape=(block, jax.ShapeDtypeStruct((n_peer, 8, chan), F32)),
            in_specs=[anywhere, vmem, vmem, anywhere, vmem],
            out_specs=(vmem, vmem),
            scratch_shapes=bufs + sems,
            compiler_params=params(0),
            name='res_first',
        )(latent, temb, res_norm, res_conv, member)

        ot = pl.pallas_call(
            functools.partial(attention, dims, count),
            out_shape=jax.ShapeDtypeStruct((chan, tok), BF16),
            in_specs=[vmem] * 5,
            out_specs=vmem,
            scratch_shapes=[
                pltpu.VMEM((n_peer, tok, chan), BF16),
                pltpu.VMEM((n_head, 2 * dim, tok), BF16),
                pltpu.VMEM((2 * tok, chan), BF16),
                pltpu.VMEM((chan, 2 * tok), BF16),
                pltpu.VMEM((2, KEY_BLK, tok), F32),
                pltpu.VMEM((n_head, 8, tok), F32),
                pltpu.VMEM((n_head, 8, tok), F32),
                pltpu.VMEM((n_head, dim, tok), F32),
                pltpu.SemaphoreType.DMA((9,)),
                pltpu.SemaphoreType.DMA((9,)),
                pltpu.SemaphoreType.DMA,
            ],
            compiler_params=params(1),
            name='attention',
        )(x1.reshape(tok, chan), every, attn_norm, proj[:3], member)

        bufs, sems = conv_scratch(2)
        return pl.pallas_call(
            functools.partial(res_second, dims, count, 1),
            out_shape=jax.ShapeDtypeStruct(latent.shape, BF16),
            in_specs=[vmem, vmem, vmem, vmem, vmem, anywhere, vmem],
            out_specs=anywhere,
            scratch_shapes=bufs + [pltpu.VMEM((own, cols, chan), BF16)] + sems,
            compiler_params=params(2),
            name='res_second',
        )(x1, ot, proj[3], temb, res_norm, res_conv, member)

    spec_x = P('dp', 'row', 'col', None)
    return jax.shard_map(run_stage, mesh=mesh, in_specs=(spec_x, P('dp', None), P(), P(), P(), P(), P()), out_specs=spec_x, check_vma=False)
```

time: 1590 us -> 190 us (0.12)
  matrix products: 407 us -> 1.85 us
  waiting for transfers between devices: 384 us -> 0 us
  local copies, waits for them, and re-layouts: 316 us -> 9.61 us
  blocking collectives: 231 us -> 0 us
  other arithmetic: 191 us -> 0 us
  Pallas kernels: 0 us -> 178 us
  starting transfers between devices: 33.5 us -> 0 us
    dot_general x68 -> x1, matrix products: 361 us -> 1.85 us  [run_stage(): jnp.einsum('bk,rkc->rbc', t_act, res_temb, preferred_element_type=F32)]
    all_gather x1 -> x0, waiting for transfers between devices: 346 us -> none  [attn_block(): kv_all = lax.all_gather(qkv_loc[1:], ('row', 'col'), axis=2, tiled=True)]
    psum x5 -> x0, blocking collectives: 231 us -> none  [group_norm(): lax.psum(part_sums, ('row', 'col')) / (n_rows * n_cols * group_ch * n_dev)]
    pallas_call x0 -> x3, Pallas kernels: none -> 178 us  [the longest x1 78.7 us: run_stage(): pl.pallas_call(functools.partial(attention, dims, count), out_shape=jax.S...]
    unnamed x44 -> x3, local copies, waits for them, and re-layouts: 177 us -> 4.16 us
    reduce_sum x48 -> x0, other arithmetic: 168 us -> none  [the longest x32 163 us: key_step(): run_sum = run_sum * rescale + jnp.sum(exp_logits, axis=-1)]
    slice x9 -> x2, local copies, waits for them, and re-layouts: 91.2 us -> 5.46 us  [the longest x1 3.35 us: run_stage(): proj[:3]]
    conv_general_dilated x4 -> x0, matrix products: 46 us -> none  [halo_conv(): lax.conv_general_dilated(padded, kernel, (1, 1), 'VALID', dimension_numbe...]
  transfers between devices with their start and end apart: 17 -> 0, of which waited for: 13 -> 0; matrix products, arithmetic and copies ran while one was open for 1% -> 0% of each run, Pallas kernels for 0% -> 0%
where the time goes in v1:
time: 190 us
  Pallas kernels  178 us (94%)
  local copies, waits for them, and re-layouts  9.61 us (5%)
    pallas_call x1, Pallas kernels, run_stage(): pl.pallas_call(functools.partial(attention, dims, count), out_shape=jax.S...  78.7 us
    pallas_call x1, Pallas kernels, run_stage(): pl.pallas_call(functools.partial(res_first, dims, count, 0), out_shape=(b...  54.5 us
    pallas_call x1, Pallas kernels, run_stage(): pl.pallas_call(functools.partial(res_second, dims, count, 1), out_shape=j...  45.1 us
    unnamed x3, local copies, waits for them, and re-layouts  4.16 us

profile of v1, /device:TPU:97, one launch (start us, length us, event | category | flops | bytes accessed | tf_op | source)
XLA Modules:
  0.0 189.8 jit_solution(17294629296676195997)
XLA Ops:
  0.0 0.0 copy-start
  0.0 1.9 %copy-done = bf16[2,1280,640]{2,1,0:T(8,128)(2,1)S(1)} copy-done((bf16[2,1280,640]{2,1,0:T(8,128)(2,1)S(1)}, bf16[2,1280,640]{2,1,0:T(8,128)(2,1)}, u32[]{:S(2)}) %copy-start) | copy-done | bytes 3276824
  1.9 1.9 convolution_bitcast_fusion.temb
  3.8 54.5 %res_first.1 = (bf16[8,96,640]{2,1,0:T(8,128)(2,1)}, f32[8,8,640]{2,1,0:T(8,128)}) custom-call(bf16[4,2,96,640]{3,2,1,0:T(8,128)(2,1)} %latent.1, f32[2,4,640]{2,1,0:T(4,128)} %convolution_bitcast_fusion.temb, bf16[2,2,2,640]{3,2,1,0:T(2,128)(2,1)} %norms.5, bf16[2,2,3,3,640,640]{5,4,3,2,1,0:T(8,128)(2,1)} %w_all.3, bf16[640,640]{1,0:T(8,128)(2,1)} %constant.5.clone.member), custom_call_target="tpu_custom_call" | custom-call | tf_op jit(solution)/shard_map/res_first/pallas_call | solution.py:511
  58.3 3.3 %slice.13 = bf16[3,10,64,640]{3,2,1,0:T(8,128)(2,1)} slice(bf16[4,10,64,640]{3,2,1,0:T(8,128)(2,1)} %bitcast.13), slice={[0:3], [0:10], [0:64], [0:640]} | slice | bytes 4915200 | tf_op jit(solution)/shard_map/slice | solution.py:541
  61.7 78.7 %attention.1.ot = bf16[640,768]{1,0:T(8,128)(2,1)} custom-call(bf16[768,640]{1,0:T(8,128)(2,1)} %bitcast.11, f32[8,8,640]{2,1,0:T(8,128)} %get-tuple-element.8.every, bf16[2,640]{1,0:T(2,128)(2,1)} %norms.4, bf16[3,640,640]{2,1,0:T(8,128)(2,1)} %bitcast.10, bf16[640,640]{1,0:T(8,128)(2,1)} %constant.5.clone.member), custom_call_target="tpu_custom_call" | custom-call | tf_op jit(solution)/shard_map/attention/pallas_call | solution.py:521
  140.4 2.1 %slice.14 = bf16[1,10,64,640]{3,2,1,0:T(8,128)(2,1)} slice(bf16[4,10,64,640]{3,2,1,0:T(8,128)(2,1)} %bitcast.14), slice={[3:4], [0:10], [0:64], [0:640]} | slice | bytes 1638400 | tf_op jit(solution)/shard_map/slice | solution.py:552
  142.5 45.1 %res_second.1 = bf16[4,2,96,640]{3,2,1,0:T(8,128)(2,1)} custom-call(bf16[8,96,640]{2,1,0:T(8,128)(2,1)} %get-tuple-element.7.x, bf16[640,768]{1,0:T(8,128)(2,1)} %attention.1.ot, bf16[640,640]{1,0:T(8,128)(2,1)} %bitcast.12, f32[2,4,640]{2,1,0:T(4,128)} %convolution_bitcast_fusion.temb, bf16[2,2,2,640]{3,2,1,0:T(2,128)(2,1)} %norms.5, ...), custom_call_target="tpu_custom_call" | custom-call | tf_op jit(solution)/shard_map/res_second/pallas_call | solution.py:544
  187.6 2.2 %copy.10 = bf16[4,2,96,640]{3,2,1,0:T(8,128)(2,1)} copy(bf16[4,2,96,640]{3,2,1,0:T(8,128)(2,1)} %res_second.1) | data formatting | bytes 1966080
Async XLA Ops:
  0.0 1.9 %copy-start = (bf16[2,1280,640]{2,1,0:T(8,128)(2,1)S(1)}, bf16[2,1280,640]{2,1,0:T(8,128)(2,1)}, u32[]{:S(2)}) copy-start(bf16[2,1280,640]{2,1,0:T(8,128)(2,1)} %param.12) | copy-start | bytes 9830404

commit v2 on v1

--- a/solution.py
+++ b/solution.py
@@ -14,6 +14,7 @@
 BF16 = jnp.bfloat16
 LOG2E = 1.4426950408889634
 KEY_BLK = 512
+QUERY_TILE = 256
 
 
 class Place:
@@ -182,9 +183,11 @@
     return vals[0:1], vals[1:2]
 
 
-def res_first(dims, count, blk, latent, temb, norms, w_all, member, x_out, stat_out, xin, hid, taps, wbuf, mine, every, hrow, colbuf, hcol, colact, wsem, ssem, rsem, xs, xr, lsem):
+def res_first(dims, count, blk, latent, t_emb, w_temb, norms, w_all, member, x_out, stat_out, xin, hid, taps, wbuf, mine, every, hrow, colbuf, hcol, colact, temb, tbuf, wsem, ssem, rsem, xs, xr, lsem):
     at = Place(dims)
     n_wait = signal_peers(at, True)
+    temb_load = pltpu.make_async_copy(w_temb.at[blk], tbuf, wsem.at[2])
+    temb_load.start()
     loads = [pltpu.make_async_copy(w_all.at[blk, j], wbuf.at[j], wsem.at[j]) for j in range(2)]
     for load in loads:
         load.start()
@@ -203,6 +206,8 @@
         def _():
             remote(latent.at[i], dst, xs.at[i], xr.at[slot], {'row': row, 'col': at.col}).start()
 
+    temb_load.wait()
+    time_terms(t_emb, tbuf, temb)
     stats = zero_stats(chan)
     for k in range(at.seg):
         row = at.half * at.seg + k
@@ -247,7 +252,7 @@
     terms = norm_terms(every.at[0], member, *norm_rows(norms.at[blk, 0]), count)
     fill_taps(at, xin, hrow.at[0], hcol.at[0], terms, taps, colact)
     loads[0].wait()
-    shift = temb[blk, pl.ds(at.img, 1), :]
+    shift = temb[pl.ds(at.img, 1), :]
 
     def first(m, stats):
         h = (conv_rows(at, taps, wbuf.at[0], m * rows) + shift).astype(BF16)
@@ -264,147 +269,186 @@
     loads[1].wait()
 
 
+def time_terms(t_emb, weights, out):
+    u = t_emb[...].astype(F32)
+    act = (u / (1.0 + jnp.exp(-u))).astype(BF16)
+    out[...] = jnp.dot(act, weights[...], preferred_element_type=F32)
+
+
 def nt(a, b):
     return lax.dot_general(a, b, (((1,), (1,)), ((), ())), preferred_element_type=F32)
 
 
-def attention(dims, count, x, every, norms, proj, member, out, xall, qm, kbuf, vbuf, sbuf, run_max, run_sum, run_out, ssem, rsem, lsem):
+def attention(dims, count, x, every, norms, proj_all, member, out, xall, qm, kbuf, vbuf, sbuf, run_max, run_sum, run_out, proj, ssem, rsem, lsem):
     at = Place(dims)
     n_wait = signal_peers(at, False)
+    load = pltpu.make_async_copy(proj_all.at[pl.ds(0, 3)], proj, lsem.at[1])
+    load.start()
     tok, chan = x.shape
     n_head = qm.shape[0]
     dim = chan // n_head
     half_tok = tok // 2
-    own_copy = pltpu.make_async_copy(x, xall.at[0], lsem)
+    own_copy = pltpu.make_async_copy(x, xall.at[0], lsem.at[0])
     own_copy.start()
     terms = norm_terms(every, member, *norm_rows(norms), count)
-
-    def normed(vals):
-        return ((vals.astype(F32) - terms[0]) * terms[1] + terms[2]).astype(BF16)
-
     right, left, mate = at.beside(1), at.beside(-1), at.partner()
     low, high = pl.ds(0, half_tok), pl.ds(half_tok, half_tok)
 
     def link(k, src, slot, device):
         return remote(src, slot, ssem.at[k], rsem.at[k], device)
 
-    to_mate = link(0, x, xall.at[1], mate)
-    to_right = link(1, x, xall.at[2], right)
-    to_left = link(2, x, xall.at[3], left)
-    left_mate = link(3, xall.at[2], xall.at[4], mate)
-    right_mate = link(4, xall.at[3], xall.at[5], mate)
-    left_right = link(5, xall.at[2, low], xall.at[6, low], right)
-    right_left = link(6, xall.at[3, high], xall.at[6, high], left)
-    far_low = link(7, xall.at[6, low], xall.at[7, low], mate)
-    far_high = link(8, xall.at[6, high], xall.at[7, high], mate)
+    low_right = link(0, x.at[low], xall.at[1, low], right)
+    high_right = link(1, x.at[high], xall.at[2, low], right)
+    high_left = link(2, x.at[high], xall.at[1, high], left)
+    low_left = link(3, x.at[low], xall.at[2, high], left)
+    far_low = link(4, xall.at[1, low], xall.at[3, low], right)
+    far_high = link(5, xall.at[1, high], xall.at[3, high], left)
+    second = pl.ds(tok, tok)
+
+    def keys_over(k):
+        return link(6 + k, kbuf.at[k, pl.ds(0, tok)], kbuf.at[k, second], mate)
+
+    def values_over(k):
+        return link(10 + k, vbuf.at[k, :, pl.ds(0, tok)], vbuf.at[k, :, second], mate)
+
     wait_peers(n_wait)
-    to_right.start()
-    to_left.start()
-    to_mate.start()
-
-    g = normed(x[...])
-    qt = nt(proj[0], g).astype(BF16)
-    zero = jnp.zeros((dim, tok), BF16)
-    for h in range(n_head):
-        mine = (h % 2) * dim
-        qm[h, mine:mine + dim, :] = qt[h * dim:(h + 1) * dim]
-        qm[h, dim - mine:2 * dim - mine, :] = zero
+    low_right.start()
+    high_left.start()
+    high_right.start()
+    low_left.start()
     run_max[...] = jnp.full(run_max.shape, -1e30, F32)
     run_sum[...] = jnp.zeros(run_sum.shape, F32)
     run_out[...] = jnp.zeros(run_out.shape, F32)
     own_copy.wait()
-
-    factor = LOG2E * dim ** -0.5
+    load.wait()
+    first_half = lax.broadcasted_iota(jnp.int32, (tok, 2 * dim), 1) < dim
+
+    def normed(vals):
+        return ((vals.astype(F32) - terms[0]) * terms[1] + terms[2]).astype(BF16)
+
+    def project(k, _):
+        @pl.when(k == 1)
+        def _():
+            low_right.wait_recv()
+            far_low.start()
+            high_left.wait_recv()
+            far_high.start()
+
+        @pl.when(k == 2)
+        def _():
+            high_right.wait_recv()
+            low_left.wait_recv()
+
+        @pl.when(k == 3)
+        def _():
+            far_low.wait_recv()
+            far_high.wait_recv()
+
+        g = normed(xall[k])
+        keys = nt(g, proj[1])
+        for p in range(n_head // 2):
+            both = keys[:, p * 2 * dim:(p + 1) * 2 * dim]
+            swapped = pltpu.roll(both, dim, 1)
+            kbuf[k, 0:tok, 4 * p * dim:(4 * p + 2) * dim] = jnp.where(first_half, both, swapped).astype(BF16)
+            kbuf[k, 0:tok, (4 * p + 2) * dim:(4 * p + 4) * dim] = jnp.where(first_half, swapped, both).astype(BF16)
+        keys_over(k).start()
+        vbuf[k, :, 0:tok] = nt(proj[2], g).astype(BF16)
+        values_over(k).start()
+        return 0
+
+    def queries():
+        qt = nt(proj[0], normed(x[...])).astype(BF16).astype(F32) * (LOG2E * dim ** -0.5)
+        hi = qt.astype(BF16)
+        rest = qt - hi.astype(F32)
+        mid = rest.astype(BF16)
+        lo = (rest - mid.astype(F32)).astype(BF16)
+        for h in range(n_head):
+            rows = slice(h * dim, (h + 1) * dim)
+            qm[h, 0:dim, :] = hi[rows]
+            qm[h, dim:2 * dim, :] = mid[rows]
+            qm[h, 2 * dim:3 * dim, :] = lo[rows]
+            qm[h, 3 * dim:4 * dim, :] = jnp.zeros((dim, tok), BF16)
+
     n_blk = 2 * tok // KEY_BLK
 
-    def scores(h, j):
-        keys = kbuf[pl.ds(j * KEY_BLK, KEY_BLK), pl.ds(pl.multiple_of((h // 2) * 2 * dim, 2 * dim), 2 * dim)]
-        return jnp.dot(keys, qm[h], preferred_element_type=F32)
-
-    def phase(k):
-        def project(b, _):
-            g = normed(xall[2 * k + b])
-            span = pl.ds(pl.multiple_of(b * tok, tok), tok)
-            kbuf[span, :] = nt(g, proj[1]).astype(BF16)
-            vbuf[:, span] = nt(proj[2], g).astype(BF16)
-            return 0
-
-        lax.fori_loop(0, 2, project, 0)
-        sbuf[0] = scores(0, 0)
-
-        def pair(p, _):
+    def attend(k):
+        keys_over(k).wait_recv()
+        values_over(k).wait_recv()
+
+        def produce(h, j, slot, cols):
+            keys = kbuf[k, pl.ds(j * KEY_BLK, KEY_BLK), pl.ds(pl.multiple_of(h * 2 * dim, 2 * dim), 2 * dim)]
+            s = jnp.dot(jnp.concatenate([keys, keys], axis=1), qm[h, :, cols], preferred_element_type=F32)
+            sbuf[slot, :, cols] = s
+            return jnp.max(s.reshape(KEY_BLK // 8, 8, QUERY_TILE), axis=0)
+
+        tiles = [slice(q, q + QUERY_TILE) for q in range(0, tok, QUERY_TILE)]
+
+        def pair(p, tops):
             for u in range(2 * n_blk):
                 h, j = 2 * p + u // n_blk, u % n_blk
                 if u + 1 < 2 * n_blk:
-                    sbuf[(u + 1) % 2] = scores(2 * p + (u + 1) // n_blk, (u + 1) % n_blk)
+                    nh, nj = 2 * p + (u + 1) // n_blk, (u + 1) % n_blk
                 else:
-                    sbuf[(u + 1) % 2] = scores(jnp.minimum(2 * p + 2, n_head - 1), 0)
-                if j == 0:
-                    m, l, acc = run_max[h, 0:1], run_sum[h, 0:1], run_out[h]
-                s = sbuf[u % 2]
-                new = jnp.maximum(m, jnp.max(s, axis=0, keepdims=True) * factor)
-                alpha = jnp.exp2(m - new)
-                w = jnp.exp2(s * factor - new)
-                l = l * alpha + jnp.sum(w, axis=0, keepdims=True)
-                vt = vbuf[pl.ds(pl.multiple_of(h * dim, dim), dim), j * KEY_BLK:(j + 1) * KEY_BLK]
-                acc = acc * alpha + jnp.dot(vt, w.astype(BF16), preferred_element_type=F32)
-                m = new
-                if j == n_blk - 1:
-                    run_max[h, 0:1], run_sum[h, 0:1], run_out[h] = m, l, acc
-            return 0
-
-        lax.fori_loop(0, n_head // 2, pair, 0)
-
-    def at_phase(k, _):
-        @pl.when(k == 0)
-        def _():
-            to_mate.wait_recv()
-
-        @pl.when(k == 1)
-        def _():
-            to_right.wait_recv()
-            left_right.start()
-            left_mate.start()
-            to_left.wait_recv()
-            right_left.start()
-            right_mate.start()
-
-        @pl.when(k == 2)
-        def _():
-            left_mate.wait_recv()
-            right_mate.wait_recv()
-            left_right.wait_recv()
-            far_low.start()
-            right_left.wait_recv()
-            far_high.start()
-
-        @pl.when(k == 3)
-        def _():
-            far_low.wait_recv()
-            far_high.wait_recv()
-
-        phase(k)
+                    nh, nj = jnp.minimum(2 * p + 2, n_head - 1), 0
+                ahead = []
+                for q, cols in enumerate(tiles):
+                    ahead.append(produce(nh, nj, (u + 1) % 2, cols))
+                    m, l, acc = run_max[h, 0:1, cols], run_sum[h, :, cols], run_out[h, :, cols]
+                    new = jnp.maximum(m, jnp.max(tops[q], axis=0, keepdims=True))
+                    alpha = jnp.exp2(m - new)
+                    w = jnp.exp2(sbuf[u % 2, :, cols] - new)
+                    run_sum[h, :, cols] = l * alpha + jnp.sum(w.reshape(KEY_BLK // 8, 8, QUERY_TILE), axis=0)
+                    run_max[h, 0:1, cols] = new
+                    vt = vbuf[k, pl.ds(pl.multiple_of(h * dim, dim), dim), j * KEY_BLK:(j + 1) * KEY_BLK]
+                    run_out[h, :, cols] = acc * alpha + jnp.dot(vt, w.astype(BF16), preferred_element_type=F32)
+                tops = ahead
+            return tuple(tops)
+
+        lax.fori_loop(0, n_head // 2, pair, tuple(produce(0, 0, 0, cols) for cols in tiles))
+
+    def step(i, _):
+        @pl.when(i > 0)
+        def _():
+            attend(i - 1)
+
+        start = jnp.minimum(i + i // 2, 4)
+        stop = jnp.minimum((i + 1) + (i + 1) // 2, 4)
+        lax.fori_loop(start, stop, project, 0)
+
+        @pl.when(i == 0)
+        def _():
+            queries()
+
         return 0
 
-    lax.fori_loop(0, 4, at_phase, 0)
-    for copy in (to_mate, to_right, to_left, left_mate, right_mate, left_right, right_left, far_low, far_high):
+    lax.fori_loop(0, 5, step, 0)
+    for copy in (low_right, high_right, high_left, low_left, far_low, far_high):
         copy.wait_send()
+    for k in range(4):
+        keys_over(k).wait_send()
+        values_over(k).wait_send()
 
     def finish(h, _):
-        out[pl.ds(pl.multiple_of(h * dim, dim), dim), :] = (run_out[h] / run_sum[h, 0:1]).astype(BF16)
+        total = jnp.sum(run_sum[h], axis=0, keepdims=True)
+        out[pl.ds(pl.multiple_of(h * dim, dim), dim), :] = (run_out[h] / total).astype(BF16)
         return 0
 
     lax.fori_loop(0, n_head, finish, 0)
 
 
-def res_second(dims, count, blk, x, ot, proj, temb, norms, w_all, member, y_out, xin, hid, taps, wbuf, mine, every, hrow, colbuf, hcol, colact, ybuf, wsem, ssem, rsem, xs, xr, lsem):
+def res_second(dims, count, blk, x, ot, proj_all, t_emb, w_temb, norms, w_all, member, y_out, xin, hid, taps, wbuf, mine, every, hrow, colbuf, hcol, colact, temb, tbuf, ybuf, proj, wsem, ssem, rsem, xs, xr, lsem):
     at = Place(dims)
     n_wait = signal_peers(at, True)
+    proj_load = pltpu.make_async_copy(proj_all.at[3], proj, wsem.at[3])
+    proj_load.start()
+    temb_load = pltpu.make_async_copy(w_temb.at[blk], tbuf, wsem.at[2])
+    temb_load.start()
     loads = [pltpu.make_async_copy(w_all.at[blk, j], wbuf.at[j], wsem.at[j]) for j in range(2)]
     for load in loads:
         load.start()
     rows, cols, chan = at.rows, at.cols, at.chan
     tile = rows * cols
+    proj_load.wait()
     add = lax.dot_general(ot[...], proj[...], (((0,), (0,)), ((), ())), preferred_element_type=F32)
     stats = zero_stats(chan)
     for m in range(at.seg):
@@ -414,6 +458,8 @@
         stats = add_stats(stats, vals)
         keep_cols(colbuf.at[0], m * rows, vals, rows, cols)
     put_stats(stats, mine.at[0], every.at[0], at)
+    temb_load.wait()
+    time_terms(t_emb, tbuf, temb)
     wait_peers(n_wait)
     swap_all(at, mine.at[0], every.at[0], ssem.at[0], rsem.at[0], xin, hrow.at[0], colbuf.at[0], hcol.at[0])
     conv_pair(at, count, blk, temb, norms, member, xin, hid, taps, wbuf, mine, every, hrow, colbuf, hcol, colact, loads, ssem, rsem)
@@ -423,7 +469,10 @@
         src = ybuf.at[pl.ds(m * rows, rows)]
         return row, pltpu.make_async_copy(src, y_out.at[at.img], lsem), remote(src, y_out.at[at.img], xs.at[m], xr.at[at.img], {'row': row, 'col': at.col})
 
-    def second(m, _):
+    near_first = (1 - ((at.img + 1) // 2) % 2 + at.half) % 2
+
+    def second(t, _):
+        m = (t + near_first * (at.seg // 2)) % at.seg
         acc = conv_rows(at, taps, wbuf.at[1], m * rows)
         y = (xin[pl.ds(m * rows, rows)].astype(F32).reshape(tile, chan) + acc).astype(BF16)
         ybuf[pl.ds(m * rows, rows)] = y.reshape(rows, cols, chan)
@@ -475,8 +524,6 @@
         count = float(n_row * rows * n_col * cols * per_group)
         group_id = np.arange(chan) // per_group
         member = jnp.asarray((group_id[:, None] == group_id[None, :]).astype(np.float32), BF16)
-        t_act = jax.nn.silu(t_emb.astype(F32)).astype(BF16)
-        temb = jnp.einsum('bk,rkc->rbc', t_act, res_temb, preferred_element_type=F32)
         proj = attn_proj.transpose(0, 1, 3, 2).reshape(4, n_head * dim, chan)
 
         vmem, anywhere = pl.BlockSpec(memory_space=pltpu.VMEM), pl.BlockSpec(memory_space=pl.ANY)
@@ -495,8 +542,10 @@
                 pltpu.VMEM((2, 2, own, chan), F32),
                 pltpu.VMEM((2, 4, own, chan), F32),
                 pltpu.VMEM((4, own, chan), F32),
+                pltpu.VMEM((n_img, chan), F32),
+                pltpu.VMEM(res_temb.shape[1:], BF16),
             ], [
-                pltpu.SemaphoreType.DMA((2,)),
+                pltpu.SemaphoreType.DMA((4,)),
                 pltpu.SemaphoreType.DMA((n_stage, n_msg)),
                 pltpu.SemaphoreType.DMA((n_stage, n_msg)),
                 pltpu.SemaphoreType.DMA((max(n_img, seg),)),
@@ -511,45 +560,46 @@
         x1, every = pl.pallas_call(
             functools.partial(res_first, dims, count, 0),
             out_shape=(block, jax.ShapeDtypeStruct((n_peer, 8, chan), F32)),
-            in_specs=[anywhere, vmem, vmem, anywhere, vmem],
+            in_specs=[anywhere, vmem, anywhere, vmem, anywhere, vmem],
             out_specs=(vmem, vmem),
             scratch_shapes=bufs + sems,
             compiler_params=params(0),
             name='res_first',
-        )(latent, temb, res_norm, res_conv, member)
+        )(latent, t_emb, res_temb, res_norm, res_conv, member)
 
         ot = pl.pallas_call(
             functools.partial(attention, dims, count),
             out_shape=jax.ShapeDtypeStruct((chan, tok), BF16),
-            in_specs=[vmem] * 5,
+            in_specs=[vmem, vmem, vmem, anywhere, vmem],
             out_specs=vmem,
             scratch_shapes=[
-                pltpu.VMEM((n_peer, tok, chan), BF16),
-                pltpu.VMEM((n_head, 2 * dim, tok), BF16),
-                pltpu.VMEM((2 * tok, chan), BF16),
-                pltpu.VMEM((chan, 2 * tok), BF16),
+                pltpu.VMEM((4, tok, chan), BF16),
+                pltpu.VMEM((n_head, 4 * dim, tok), BF16),
+                pltpu.VMEM((4, 2 * tok, 2 * chan), BF16),
+                pltpu.VMEM((4, chan, 2 * tok), BF16),
                 pltpu.VMEM((2, KEY_BLK, tok), F32),
                 pltpu.VMEM((n_head, 8, tok), F32),
                 pltpu.VMEM((n_head, 8, tok), F32),
                 pltpu.VMEM((n_head, dim, tok), F32),
-                pltpu.SemaphoreType.DMA((9,)),
-                pltpu.SemaphoreType.DMA((9,)),
-                pltpu.SemaphoreType.DMA,
+                pltpu.VMEM((3, chan, chan), BF16),
+                pltpu.SemaphoreType.DMA((14,)),
+                pltpu.SemaphoreType.DMA((14,)),
+                pltpu.SemaphoreType.DMA((2,)),
             ],
             compiler_params=params(1),
             name='attention',
-        )(x1.reshape(tok, chan), every, attn_norm, proj[:3], member)
+        )(x1.reshape(tok, chan), every, attn_norm, proj, member)
 
         bufs, sems = conv_scratch(2)
         return pl.pallas_call(
             functools.partial(res_second, dims, count, 1),
             out_shape=jax.ShapeDtypeStruct(latent.shape, BF16),
-            in_specs=[vmem, vmem, vmem, vmem, vmem, anywhere, vmem],
+            in_specs=[vmem, vmem, anywhere, vmem, anywhere, vmem, anywhere, vmem],
             out_specs=anywhere,
-            scratch_shapes=bufs + [pltpu.VMEM((own, cols, chan), BF16)] + sems,
+            scratch_shapes=bufs + [pltpu.VMEM((own, cols, chan), BF16), pltpu.VMEM((chan, chan), BF16)] + sems,
             compiler_params=params(2),
             name='res_second',
-        )(x1, ot, proj[3], temb, res_norm, res_conv, member)
+        )(x1, ot, proj, t_emb, res_temb, res_norm, res_conv, member)
 
     spec_x = P('dp', 'row', 'col', None)
     return jax.shard_map(run_stage, mesh=mesh, in_specs=(spec_x, P('dp', None), P(), P(), P(), P(), P()), out_specs=spec_x, check_vma=False)

time: 190 us -> 173 us (0.911)
  local copies, waits for them, and re-layouts: 9.61 us -> 2.23 us
  Pallas kernels: 178 us -> 171 us
    pallas_call x1, Pallas kernels: 78.7 us -> 69.5 us  [run_stage(): pl.pallas_call(functools.partial(attention, dims, count), out_shape=jax.S...]
    slice x2 -> x0, local copies, waits for them, and re-layouts: 5.46 us -> none  [the longest x1 3.35 us: run_stage(): proj[:3]]
    unnamed x3 -> x1, local copies, waits for them, and re-layouts: 4.16 us -> 2.23 us
where the time goes in v2:
time: 173 us
  Pallas kernels  171 us (99%)
  local copies, waits for them, and re-layouts  2.23 us (1%)
    pallas_call x1, Pallas kernels, run_stage(): pl.pallas_call(functools.partial(attention, dims, count), out_shape=jax.S...  69.5 us
    pallas_call x1, Pallas kernels, run_stage(): pl.pallas_call(functools.partial(res_first, dims, count, 0), out_shape=(b...  54.5 us
    pallas_call x1, Pallas kernels, run_stage(): pl.pallas_call(functools.partial(res_second, dims, count, 1), out_shape=j...  46.7 us

profile of v2, /device:TPU:97, one launch (start us, length us, event | category | flops | bytes accessed | tf_op | source)
XLA Modules:
  0.0 173.0 jit_solution(4814289774207987084)
XLA Ops:
  0.0 54.5 %res_first.1 = (bf16[8,96,640]{2,1,0:T(8,128)(2,1)}, f32[8,8,640]{2,1,0:T(8,128)}) custom-call(bf16[4,2,96,640]{3,2,1,0:T(8,128)(2,1)} %latent.1, bf16[4,1280]{1,0:T(4,128)(2,1)} %t_emb.3, bf16[2,1280,640]{2,1,0:T(8,128)(2,1)} %w_temb.3, bf16[2,2,2,640]{3,2,1,0:T(2,128)(2,1)} %norms.5, bf16[2,2,3,3,640,640]{5,4,3,2,1,0:T(8,128)(2,1)} %w_all.3, ...), custom_call_target="tpu_custom_call" | custom-call | tf_op jit(solution)/shard_map/res_first/pallas_call | solution.py:560
  54.6 69.5 %attention.1.ot = bf16[640,768]{1,0:T(8,128)(2,1)} custom-call(bf16[768,640]{1,0:T(8,128)(2,1)} %bitcast.6, f32[8,8,640]{2,1,0:T(8,128)} %get-tuple-element.8.every, bf16[2,640]{1,0:T(2,128)(2,1)} %norms.4, bf16[4,640,640]{2,1,0:T(8,128)(2,1)} %bitcast.4, bf16[640,640]{1,0:T(8,128)(2,1)} %constant.2.clone.member), custom_call_target="tpu_custom_call" | custom-call | tf_op jit(solution)/shard_map/attention/pallas_call | solution.py:570
  124.1 46.7 %res_second.1 = bf16[4,2,96,640]{3,2,1,0:T(8,128)(2,1)} custom-call(bf16[8,96,640]{2,1,0:T(8,128)(2,1)} %get-tuple-element.7.x, bf16[640,768]{1,0:T(8,128)(2,1)} %attention.1.ot, bf16[4,640,640]{2,1,0:T(8,128)(2,1)} %bitcast.5, bf16[4,1280]{1,0:T(4,128)(2,1)} %t_emb.3, bf16[2,1280,640]{2,1,0:T(8,128)(2,1)} %w_temb.3, bf16[2,2,2,640]{3,2,1,0:T(2,128)(2,1)} %norms.5, ...), custom_call_target="tpu_custom_call" | custom-call | tf_op jit(solution)/shard_map/res_second/pallas_call | solution.py:594
  170.8 2.2 %copy.10 = bf16[4,2,96,640]{3,2,1,0:T(8,128)(2,1)} copy(bf16[4,2,96,640]{3,2,1,0:T(8,128)(2,1)} %res_second.1) | data formatting | bytes 1966080

commit v3 on v2

--- a/solution.py
+++ b/solution.py
@@ -85,40 +85,50 @@
     return out
 
 
-def put_stats(stats, mine, every, at):
+def split_dot(vals, matrix):
+    high = vals.astype(BF16).astype(F32)
+    mid = (vals - high).astype(BF16).astype(F32)
+    low = (vals - high - mid).astype(BF16).astype(F32)
+    stacked = jnp.concatenate([high, mid, low, jnp.zeros_like(low)], axis=0).astype(BF16)
+    out = jnp.dot(stacked, matrix, preferred_element_type=F32)
+    return out[0:8] + out[8:16] + out[16:24]
+
+
+def two_rows(first, second, shape):
+    idx = lax.broadcasted_iota(jnp.int32, shape, 0)
+    return jnp.where(idx == 0, first, jnp.where(idx == 1, second, 0.0))
+
+
+def put_stats(stats, mine, every, gather, at):
     s1 = jnp.sum(stats[0], axis=0, keepdims=True)
     s2 = jnp.sum(stats[1], axis=0, keepdims=True)
-    idx = lax.broadcasted_iota(jnp.int32, mine.shape, 0)
-    both = jnp.where(idx == 0, s1, jnp.where(idx == 1, s2, 0.0))
-    mine[...] = both
-    every[at.me] = both
-
-
-def swap_all(at, mine, every, ssem, rsem, full=None, hrow=None, colbuf=None, hcol=None):
-    copies = [] if full is None else halo_copies(at, full, hrow, colbuf, hcol, ssem, rsem)
-    copies += stat_copies(at, mine, every, ssem, rsem)
-    for send, _ in copies:
+    groups = split_dot(two_rows(s1, s2, stats[0].shape), gather[...])
+    mine[...] = groups
+    every[at.me] = groups
+
+
+def swap_all(at, stats, mine, every, gather, ssem, rsem, full=None, hrow=None, colbuf=None, hcol=None):
+    halos = [] if full is None else halo_copies(at, full, hrow, colbuf, hcol, ssem, rsem)
+    for send, _ in halos:
         send.start()
-    for _, recv in copies:
+    put_stats(stats, mine, every, gather, at)
+    sums = stat_copies(at, mine, every, ssem, rsem)
+    for send, _ in sums:
+        send.start()
+    for _, recv in sums + halos:
         recv.wait_recv()
-    for send, _ in copies:
+    for send, _ in sums + halos:
         send.wait_send()
 
 
-def norm_terms(every, member, scale, shift, count):
+def norm_terms(every, spread, scale, shift, count):
     total = every[0]
     for slot in range(1, every.shape[0]):
         total = total + every[slot]
-    high = total.astype(BF16).astype(F32)
-    mid = (total - high).astype(BF16).astype(F32)
-    low = (total - high - mid).astype(BF16).astype(F32)
-    stacked = jnp.concatenate([high, mid, low, jnp.zeros_like(low)], axis=0).astype(BF16)
-    n = total.shape[0]
-    summed = jnp.dot(stacked, member[...], preferred_element_type=F32)
-    sums = summed[0:n] + summed[n:2 * n] + summed[2 * n:3 * n]
-    mean = sums[0:1] / count
-    var = sums[1:2] / count - mean * mean
-    return mean, lax.rsqrt(var + EPS) * scale, shift
+    mean = total[0:1] / count
+    inv = lax.rsqrt(total[1:2] / count - mean * mean + EPS)
+    wide = split_dot(two_rows(mean, inv, total.shape), spread[...])
+    return wide[0:1], wide[1:2] * scale, shift
 
 
 def activate(x, terms):
@@ -183,15 +193,7 @@
     return vals[0:1], vals[1:2]
 
 
-def res_first(dims, count, blk, latent, t_emb, w_temb, norms, w_all, member, x_out, stat_out, xin, hid, taps, wbuf, mine, every, hrow, colbuf, hcol, colact, temb, tbuf, wsem, ssem, rsem, xs, xr, lsem):
-    at = Place(dims)
-    n_wait = signal_peers(at, True)
-    temb_load = pltpu.make_async_copy(w_temb.at[blk], tbuf, wsem.at[2])
-    temb_load.start()
-    loads = [pltpu.make_async_copy(w_all.at[blk, j], wbuf.at[j], wsem.at[j]) for j in range(2)]
-    for load in loads:
-        load.start()
-    wait_peers(n_wait)
+def spread_images(at, latent, xin, xs, xr, lsem, colbuf):
     target_half, slot = at.row // at.seg, at.row % at.seg
     rows, cols, chan = at.rows, at.cols, at.chan
     for i in range(at.n_img):
@@ -206,8 +208,7 @@
         def _():
             remote(latent.at[i], dst, xs.at[i], xr.at[slot], {'row': row, 'col': at.col}).start()
 
-    temb_load.wait()
-    time_terms(t_emb, tbuf, temb)
+    yield
     stats = zero_stats(chan)
     for k in range(at.seg):
         row = at.half * at.seg + k
@@ -223,9 +224,8 @@
 
         vals = xin[k * rows:(k + 1) * rows].astype(F32).reshape(rows * cols, chan)
         stats = add_stats(stats, vals)
-        keep_cols(colbuf.at[0], k * rows, vals, rows, cols)
-    put_stats(stats, mine.at[0], every.at[0], at)
-    swap_all(at, mine.at[0], every.at[0], ssem.at[0], rsem.at[0], xin, hrow.at[0], colbuf.at[0], hcol.at[0])
+        keep_cols(colbuf, k * rows, vals, rows, cols)
+    yield stats
     for i in range(at.n_img):
         row = i * at.halves + target_half
 
@@ -233,24 +233,13 @@
         def _():
             remote(latent.at[i], xin.at[pl.ds(slot * rows, rows)], xs.at[i], xr.at[slot], {'row': row, 'col': at.col}).wait_send()
 
-    conv_pair(at, count, blk, temb, norms, member, xin, hid, taps, wbuf, mine, every, hrow, colbuf, hcol, colact, loads, ssem, rsem)
-
-    def second(m, stats):
-        acc = conv_rows(at, taps, wbuf.at[1], m * rows)
-        y = (xin[pl.ds(m * rows, rows)].astype(F32).reshape(rows * cols, chan) + acc).astype(BF16)
-        x_out[pl.ds(m * rows, rows)] = y.reshape(rows, cols, chan)
-        return add_stats(stats, y.astype(F32))
-
-    stats = lax.fori_loop(0, at.seg, second, zero_stats(chan))
-    put_stats(stats, mine.at[2], every.at[2], at)
-    swap_all(at, mine.at[2], every.at[2], ssem.at[2], rsem.at[2])
-    stat_out[...] = every[2]
-
-
-def conv_pair(at, count, blk, temb, norms, member, xin, hid, taps, wbuf, mine, every, hrow, colbuf, hcol, colact, loads, ssem, rsem):
+    yield
+
+
+def conv_pair(at, count, blk, stage, halo, temb, norms, gather, spread, xin, hid, taps, wbuf, mine, every, hrow, colbuf, hcol, colact, loads, after_first, ssem, rsem):
     rows, cols, chan = at.rows, at.cols, at.chan
-    terms = norm_terms(every.at[0], member, *norm_rows(norms.at[blk, 0]), count)
-    fill_taps(at, xin, hrow.at[0], hcol.at[0], terms, taps, colact)
+    terms = norm_terms(every.at[stage], spread, *norm_rows(norms.at[blk, 0]), count)
+    fill_taps(at, xin, hrow.at[halo], hcol.at[halo], terms, taps, colact)
     loads[0].wait()
     shift = temb[pl.ds(at.img, 1), :]
 
@@ -258,14 +247,15 @@
         h = (conv_rows(at, taps, wbuf.at[0], m * rows) + shift).astype(BF16)
         hid[pl.ds(m * rows, rows)] = h.reshape(rows, cols, chan)
         vals = h.astype(F32)
-        keep_cols(colbuf.at[1], m * rows, vals, rows, cols)
+        keep_cols(colbuf.at[halo + 1], m * rows, vals, rows, cols)
         return add_stats(stats, vals)
 
     stats = lax.fori_loop(0, at.seg, first, zero_stats(chan))
-    put_stats(stats, mine.at[1], every.at[1], at)
-    swap_all(at, mine.at[1], every.at[1], ssem.at[1], rsem.at[1], hid, hrow.at[1], colbuf.at[1], hcol.at[1])
-    terms = norm_terms(every.at[1], member, *norm_rows(norms.at[blk, 1]), count)
-    fill_taps(at, hid, hrow.at[1], hcol.at[1], terms, taps, colact)
+    if after_first is not None:
+        after_first.start()
+    swap_all(at, stats, mine.at[stage + 1], every.at[stage + 1], gather, ssem.at[stage + 1], rsem.at[stage + 1], hid, hrow.at[halo + 1], colbuf.at[halo + 1], hcol.at[halo + 1])
+    terms = norm_terms(every.at[stage + 1], spread, *norm_rows(norms.at[blk, 1]), count)
+    fill_taps(at, hid, hrow.at[halo + 1], hcol.at[halo + 1], terms, taps, colact)
     loads[1].wait()
 
 
@@ -279,18 +269,13 @@
     return lax.dot_general(a, b, (((1,), (1,)), ((), ())), preferred_element_type=F32)
 
 
-def attention(dims, count, x, every, norms, proj_all, member, out, xall, qm, kbuf, vbuf, sbuf, run_max, run_sum, run_out, proj, ssem, rsem, lsem):
-    at = Place(dims)
-    n_wait = signal_peers(at, False)
-    load = pltpu.make_async_copy(proj_all.at[pl.ds(0, 3)], proj, lsem.at[1])
-    load.start()
-    tok, chan = x.shape
+def attention(at, count, every, norms, spread, proj, load, out, xall, kbuf, vbuf, ssem, rsem, qm, sbuf, run_max, run_sum, run_out):
+    _, tok, chan = xall.shape
     n_head = qm.shape[0]
     dim = chan // n_head
     half_tok = tok // 2
-    own_copy = pltpu.make_async_copy(x, xall.at[0], lsem.at[0])
-    own_copy.start()
-    terms = norm_terms(every, member, *norm_rows(norms), count)
+    x = xall.at[0]
+    terms = norm_terms(every, spread, *norm_rows(norms), count)
     right, left, mate = at.beside(1), at.beside(-1), at.partner()
     low, high = pl.ds(0, half_tok), pl.ds(half_tok, half_tok)
 
@@ -311,7 +296,6 @@
     def values_over(k):
         return link(10 + k, vbuf.at[k, :, pl.ds(0, tok)], vbuf.at[k, :, second], mate)
 
-    wait_peers(n_wait)
     low_right.start()
     high_left.start()
     high_right.start()
@@ -319,7 +303,6 @@
     run_max[...] = jnp.full(run_max.shape, -1e30, F32)
     run_sum[...] = jnp.zeros(run_sum.shape, F32)
     run_out[...] = jnp.zeros(run_out.shape, F32)
-    own_copy.wait()
     load.wait()
     first_half = lax.broadcasted_iota(jnp.int32, (tok, 2 * dim), 1) < dim
 
@@ -436,33 +419,72 @@
     lax.fori_loop(0, n_head, finish, 0)
 
 
-def res_second(dims, count, blk, x, ot, proj_all, t_emb, w_temb, norms, w_all, member, y_out, xin, hid, taps, wbuf, mine, every, hrow, colbuf, hcol, colact, temb, tbuf, ybuf, proj, wsem, ssem, rsem, xs, xr, lsem):
+def stage(dims, count, n_head, latent, t_emb, w_temb, norms, w_all, a_norms, proj_all, gather, spread, y_out, xin, hid, wbuf, mine, every, hrow, colbuf, hcol, colact, temb, tbuf, proj, ot, xall, kbuf, vbuf, wsem, ssem, rsem, xs, xr, ys, yr, lsem, asend, arecv):
     at = Place(dims)
     n_wait = signal_peers(at, True)
-    proj_load = pltpu.make_async_copy(proj_all.at[3], proj, wsem.at[3])
-    proj_load.start()
-    temb_load = pltpu.make_async_copy(w_temb.at[blk], tbuf, wsem.at[2])
-    temb_load.start()
-    loads = [pltpu.make_async_copy(w_all.at[blk, j], wbuf.at[j], wsem.at[j]) for j in range(2)]
-    for load in loads:
-        load.start()
     rows, cols, chan = at.rows, at.cols, at.chan
     tile = rows * cols
-    proj_load.wait()
-    add = lax.dot_general(ot[...], proj[...], (((0,), (0,)), ((), ())), preferred_element_type=F32)
+    tok = tile * at.seg
+    loads = [pltpu.make_async_copy(w_all.at[blk, j], wbuf.at[j], wsem.at[2 * blk + j]) for blk in range(2) for j in range(2)]
+    temb_loads = [pltpu.make_async_copy(w_temb.at[blk], tbuf, wsem.at[4 + blk]) for blk in range(2)]
+    proj_load = pltpu.make_async_copy(proj_all, proj, wsem.at[6])
+    wait_peers(n_wait)
+    images = spread_images(at, latent, xin, xs, xr, lsem, colbuf.at[0])
+    next(images)
+    temb_loads[0].start()
+    loads[0].start()
+    loads[1].start()
+    proj_load.start()
+    temb_loads[0].wait()
+    time_terms(t_emb, tbuf, temb)
+    temb_loads[1].start()
+    stats = next(images)
+    swap_all(at, stats, mine.at[0], every.at[0], gather, ssem.at[0], rsem.at[0], xin, hrow.at[0], colbuf.at[0], hcol.at[0])
+    next(images)
+    tap_shape = pltpu.VMEM((rows * at.seg + 2, cols, 3 * chan), BF16)
+
+    def first_block(taps):
+        conv_pair(at, count, 0, 0, 0, temb, norms, gather, spread, xin, hid, taps, wbuf, mine, every, hrow, colbuf, hcol, colact, loads[0:2], loads[2], ssem, rsem)
+
+        def second(m, stats):
+            acc = conv_rows(at, taps, wbuf.at[1], m * rows)
+            y = (xin[pl.ds(m * rows, rows)].astype(F32).reshape(tile, chan) + acc).astype(BF16)
+            xall[0, pl.ds(m * tile, tile)] = y
+            return add_stats(stats, y.astype(F32))
+
+        stats = lax.fori_loop(0, at.seg, second, zero_stats(chan))
+        loads[3].start()
+        swap_all(at, stats, mine.at[2], every.at[2], gather, ssem.at[2], rsem.at[2])
+
+    pl.run_scoped(first_block, tap_shape)
+    dim = chan // n_head
+    pl.run_scoped(
+        functools.partial(attention, at, count, every.at[2], a_norms, spread, proj, proj_load, ot, xall, kbuf, vbuf, asend, arecv),
+        pltpu.VMEM((n_head, 4 * dim, tok), BF16),
+        pltpu.VMEM((2, KEY_BLK, tok), F32),
+        pltpu.VMEM((n_head, 8, tok), F32),
+        pltpu.VMEM((n_head, 8, tok), F32),
+        pltpu.VMEM((n_head, dim, tok), F32),
+    )
+    temb_loads[1].wait()
+    time_terms(t_emb, tbuf, temb)
+    pl.run_scoped(functools.partial(second_block, at, count, norms, gather, spread, y_out, xin, hid, wbuf, mine, every, hrow, colbuf, hcol, colact, temb, proj, ot, xall, loads, ssem, rsem, ys, yr, lsem), tap_shape)
+
+
+def second_block(at, count, norms, gather, spread, y_out, xin, hid, wbuf, mine, every, hrow, colbuf, hcol, colact, temb, proj, ot, xall, loads, ssem, rsem, xs, xr, lsem, taps):
+    rows, cols, chan = at.rows, at.cols, at.chan
+    tile = rows * cols
+    add = lax.dot_general(ot[...], proj[3], (((0,), (0,)), ((), ())), preferred_element_type=F32)
     stats = zero_stats(chan)
     for m in range(at.seg):
-        y = (x[m * rows:(m + 1) * rows].astype(F32).reshape(tile, chan) + add[m * tile:(m + 1) * tile]).astype(BF16)
+        y = (xall[0, m * tile:(m + 1) * tile].astype(F32) + add[m * tile:(m + 1) * tile]).astype(BF16)
         xin[m * rows:(m + 1) * rows] = y.reshape(rows, cols, chan)
         vals = y.astype(F32)
         stats = add_stats(stats, vals)
-        keep_cols(colbuf.at[0], m * rows, vals, rows, cols)
-    put_stats(stats, mine.at[0], every.at[0], at)
-    temb_load.wait()
-    time_terms(t_emb, tbuf, temb)
-    wait_peers(n_wait)
-    swap_all(at, mine.at[0], every.at[0], ssem.at[0], rsem.at[0], xin, hrow.at[0], colbuf.at[0], hcol.at[0])
-    conv_pair(at, count, blk, temb, norms, member, xin, hid, taps, wbuf, mine, every, hrow, colbuf, hcol, colact, loads, ssem, rsem)
+        keep_cols(colbuf.at[2], m * rows, vals, rows, cols)
+    swap_all(at, stats, mine.at[3], every.at[3], gather, ssem.at[3], rsem.at[3], xin, hrow.at[2], colbuf.at[2], hcol.at[2])
+    conv_pair(at, count, 1, 3, 2, temb, norms, gather, spread, xin, hid, taps, wbuf, mine, every, hrow, colbuf, hcol, colact, loads[2:4], None, ssem, rsem)
+    ybuf = hid
 
     def back(m):
         row = at.half * at.seg + m
@@ -523,83 +545,47 @@
         per_group = chan // GROUPS
         count = float(n_row * rows * n_col * cols * per_group)
         group_id = np.arange(chan) // per_group
-        member = jnp.asarray((group_id[:, None] == group_id[None, :]).astype(np.float32), BF16)
+        member = (group_id[:, None] == np.arange(128)[None, :]).astype(np.float32)
         proj = attn_proj.transpose(0, 1, 3, 2).reshape(4, n_head * dim, chan)
-
+        n_msg = n_peer - 1 + 5
+        n_stage = 5
         vmem, anywhere = pl.BlockSpec(memory_space=pltpu.VMEM), pl.BlockSpec(memory_space=pl.ANY)
-        block = jax.ShapeDtypeStruct((own, cols, chan), BF16)
-
-        def conv_scratch(n_stage):
-            n_msg = n_peer - 1 + 5
-            return [
+        return pl.pallas_call(
+            functools.partial(stage, dims, count, n_head),
+            out_shape=jax.ShapeDtypeStruct(latent.shape, BF16),
+            in_specs=[anywhere, vmem, anywhere, vmem, anywhere, vmem, anywhere, vmem, vmem],
+            out_specs=anywhere,
+            scratch_shapes=[
                 pltpu.VMEM((own, cols, chan), BF16),
                 pltpu.VMEM((own, cols, chan), BF16),
-                pltpu.VMEM((own + 2, cols, 3 * chan), BF16),
                 pltpu.VMEM((2, 3, 3, chan, chan), BF16),
-                pltpu.VMEM((n_stage, 8, chan), F32),
-                pltpu.VMEM((n_stage, n_peer, 8, chan), F32),
-                pltpu.VMEM((2, cols, chan), BF16),
-                pltpu.VMEM((2, 2, own, chan), F32),
-                pltpu.VMEM((2, 4, own, chan), F32),
+                pltpu.VMEM((n_stage, 8, 128), F32),
+                pltpu.VMEM((n_stage, n_peer, 8, 128), F32),
+                pltpu.VMEM((4, cols, chan), BF16),
+                pltpu.VMEM((4, 2, own, chan), F32),
+                pltpu.VMEM((4, 4, own, chan), F32),
                 pltpu.VMEM((4, own, chan), F32),
                 pltpu.VMEM((n_img, chan), F32),
                 pltpu.VMEM(res_temb.shape[1:], BF16),
-            ], [
-                pltpu.SemaphoreType.DMA((4,)),
+                pltpu.VMEM((4, n_head * dim, chan), BF16),
+                pltpu.VMEM((n_head * dim, tok), BF16),
+                pltpu.VMEM((4, tok, chan), BF16),
+                pltpu.VMEM((4, 2 * tok, 2 * chan), BF16),
+                pltpu.VMEM((4, chan, 2 * tok), BF16),
+                pltpu.SemaphoreType.DMA((7,)),
                 pltpu.SemaphoreType.DMA((n_stage, n_msg)),
                 pltpu.SemaphoreType.DMA((n_stage, n_msg)),
-                pltpu.SemaphoreType.DMA((max(n_img, seg),)),
-                pltpu.SemaphoreType.DMA((max(n_img, seg),)),
+                pltpu.SemaphoreType.DMA((n_img,)),
+                pltpu.SemaphoreType.DMA((seg,)),
+                pltpu.SemaphoreType.DMA((seg,)),
+                pltpu.SemaphoreType.DMA((n_img,)),
                 pltpu.SemaphoreType.DMA,
-            ]
-
-        def params(cid):
-            return pltpu.CompilerParams(collective_id=cid, has_side_effects=True, vmem_limit_bytes=60 << 20)
-
-        bufs, sems = conv_scratch(3)
-        x1, every = pl.pallas_call(
-            functools.partial(res_first, dims, count, 0),
-            out_shape=(block, jax.ShapeDtypeStruct((n_peer, 8, chan), F32)),
-            in_specs=[anywhere, vmem, anywhere, vmem, anywhere, vmem],
-            out_specs=(vmem, vmem),
-            scratch_shapes=bufs + sems,
-            compiler_params=params(0),
-            name='res_first',
-        )(latent, t_emb, res_temb, res_norm, res_conv, member)
-
-        ot = pl.pallas_call(
-            functools.partial(attention, dims, count),
-            out_shape=jax.ShapeDtypeStruct((chan, tok), BF16),
-            in_specs=[vmem, vmem, vmem, anywhere, vmem],
-            out_specs=vmem,
-            scratch_shapes=[
-                pltpu.VMEM((4, tok, chan), BF16),
-                pltpu.VMEM((n_head, 4 * dim, tok), BF16),
-                pltpu.VMEM((4, 2 * tok, 2 * chan), BF16),
-                pltpu.VMEM((4, chan, 2 * tok), BF16),
-                pltpu.VMEM((2, KEY_BLK, tok), F32),
-                pltpu.VMEM((n_head, 8, tok), F32),
-                pltpu.VMEM((n_head, 8, tok), F32),
-                pltpu.VMEM((n_head, dim, tok), F32),
-                pltpu.VMEM((3, chan, chan), BF16),
                 pltpu.SemaphoreType.DMA((14,)),
                 pltpu.SemaphoreType.DMA((14,)),
-                pltpu.SemaphoreType.DMA((2,)),
             ],
-            compiler_params=params(1),
-            name='attention',
-        )(x1.reshape(tok, chan), every, attn_norm, proj, member)
-
-        bufs, sems = conv_scratch(2)
-        return pl.pallas_call(
-            functools.partial(res_second, dims, count, 1),
-            out_shape=jax.ShapeDtypeStruct(latent.shape, BF16),
-            in_specs=[vmem, vmem, anywhere, vmem, anywhere, vmem, anywhere, vmem],
-            out_specs=anywhere,
-            scratch_shapes=bufs + [pltpu.VMEM((own, cols, chan), BF16), pltpu.VMEM((chan, chan), BF16)] + sems,
-            compiler_params=params(2),
-            name='res_second',
-        )(x1, ot, proj, t_emb, res_temb, res_norm, res_conv, member)
+            compiler_params=pltpu.CompilerParams(collective_id=0, has_side_effects=True, vmem_limit_bytes=67043328),
+            name='unet_stage',
+        )(latent, t_emb, res_temb, res_norm, res_conv, attn_norm, proj, jnp.asarray(member, BF16), jnp.asarray(member.T.copy(), BF16))
 
     spec_x = P('dp', 'row', 'col', None)
     return jax.shard_map(run_stage, mesh=mesh, in_specs=(spec_x, P('dp', None), P(), P(), P(), P(), P()), out_specs=spec_x, check_vma=False)

time: 173 us -> 161 us (0.931)
  Pallas kernels: 171 us -> 158 us
    pallas_call x3 -> x1, Pallas kernels: 171 us -> 158 us  [run_stage(): pl.pallas_call(functools.partial(stage, dims, count, n_head), out_shape=j...]
where the time goes in v3:
time: 161 us; the launch traced here: 160 us
  Pallas kernels  158 us (98%)
  local copies, waits for them, and re-layouts  2.23 us (1%)
    pallas_call x1, Pallas kernels, run_stage(): pl.pallas_call(functools.partial(stage, dims, count, n_head), out_shape=j...  158 us

profile of v3, /device:TPU:97, one launch (start us, length us, event | category | flops | bytes accessed | tf_op | source)
XLA Modules:
  0.0 160.4 jit_solution(2746122687594941977)
XLA Ops:
  0.0 158.1 %unet_stage.1 = bf16[4,2,96,640]{3,2,1,0:T(8,128)(2,1)} custom-call(bf16[4,2,96,640]{3,2,1,0:T(8,128)(2,1)} %latent.1, bf16[4,1280]{1,0:T(4,128)(2,1)} %t_emb.1, bf16[2,1280,640]{2,1,0:T(8,128)(2,1)} %w_temb.1, bf16[2,2,2,640]{3,2,1,0:T(2,128)(2,1)} %norms.1, bf16[2,2,3,3,640,640]{5,4,3,2,1,0:T(8,128)(2,1)} %w_all.1, bf16[2,640]{1,0:T(2,128)(2,1)} %a_norms.1, ...), custom_call_target="tpu_custom_call" | custom-call | tf_op jit(solution)/shard_map/unet_stage/pallas_call | solution.py:553
  158.2 2.2 %copy.11 = bf16[4,2,96,640]{3,2,1,0:T(8,128)(2,1)} copy(bf16[4,2,96,640]{3,2,1,0:T(8,128)(2,1)} %unet_stage.1) | data formatting | bytes 1966080

commit v4 on v3

--- a/solution.py
+++ b/solution.py
@@ -15,6 +15,7 @@
 LOG2E = 1.4426950408889634
 KEY_BLK = 512
 QUERY_TILE = 256
+HEADS_PER_STEP = 5
 
 
 class Place:
@@ -107,7 +108,7 @@
     every[at.me] = groups
 
 
-def swap_all(at, stats, mine, every, gather, ssem, rsem, full=None, hrow=None, colbuf=None, hcol=None):
+def swap_all(at, stats, mine, every, gather, ssem, rsem, full=None, hrow=None, colbuf=None, hcol=None, behind=()):
     halos = [] if full is None else halo_copies(at, full, hrow, colbuf, hcol, ssem, rsem)
     for send, _ in halos:
         send.start()
@@ -115,6 +116,8 @@
     sums = stat_copies(at, mine, every, ssem, rsem)
     for send, _ in sums:
         send.start()
+    for copy in behind:
+        copy.start()
     for _, recv in sums + halos:
         recv.wait_recv()
     for send, _ in sums + halos:
@@ -133,8 +136,8 @@
 
 def activate(x, terms):
     mean, scale, shift = terms
-    u = (x - mean) * scale + shift
-    return u / (1.0 + jnp.exp(-u))
+    half = ((x - mean) * scale + shift) * 0.5
+    return half + half * jnp.tanh(half)
 
 
 def add_stats(stats, vals):
@@ -269,25 +272,27 @@
     return lax.dot_general(a, b, (((1,), (1,)), ((), ())), preferred_element_type=F32)
 
 
-def attention(at, count, every, norms, spread, proj, load, out, xall, kbuf, vbuf, ssem, rsem, qm, sbuf, run_max, run_sum, run_out):
+def gather_links(at, xall, ssem, rsem):
+    half_tok = xall.shape[1] // 2
+    right, left = at.beside(1), at.beside(-1)
+    low, high = pl.ds(0, half_tok), pl.ds(half_tok, half_tok)
+    x = xall.at[0]
+    ends = [(x.at[low], xall.at[1, low], right), (x.at[high], xall.at[2, low], right), (x.at[high], xall.at[1, high], left), (x.at[low], xall.at[2, high], left), (xall.at[1, low], xall.at[3, low], right), (xall.at[1, high], xall.at[3, high], left)]
+    return [remote(src, dst, ssem.at[k], rsem.at[k], device) for k, (src, dst, device) in enumerate(ends)]
+
+
+def attention(at, count, every, norms, spread, proj, load, meanwhile, out, xall, kbuf, vbuf, ssem, rsem, qm, sbuf, run_max, run_sum, run_out):
     _, tok, chan = xall.shape
     n_head = qm.shape[0]
     dim = chan // n_head
-    half_tok = tok // 2
     x = xall.at[0]
     terms = norm_terms(every, spread, *norm_rows(norms), count)
-    right, left, mate = at.beside(1), at.beside(-1), at.partner()
-    low, high = pl.ds(0, half_tok), pl.ds(half_tok, half_tok)
+    mate = at.partner()
 
     def link(k, src, slot, device):
         return remote(src, slot, ssem.at[k], rsem.at[k], device)
 
-    low_right = link(0, x.at[low], xall.at[1, low], right)
-    high_right = link(1, x.at[high], xall.at[2, low], right)
-    high_left = link(2, x.at[high], xall.at[1, high], left)
-    low_left = link(3, x.at[low], xall.at[2, high], left)
-    far_low = link(4, xall.at[1, low], xall.at[3, low], right)
-    far_high = link(5, xall.at[1, high], xall.at[3, high], left)
+    low_right, high_right, high_left, low_left, far_low, far_high = gather_links(at, xall, ssem, rsem)
     second = pl.ds(tok, tok)
 
     def keys_over(k):
@@ -296,13 +301,6 @@
     def values_over(k):
         return link(10 + k, vbuf.at[k, :, pl.ds(0, tok)], vbuf.at[k, :, second], mate)
 
-    low_right.start()
-    high_left.start()
-    high_right.start()
-    low_left.start()
-    run_max[...] = jnp.full(run_max.shape, -1e30, F32)
-    run_sum[...] = jnp.zeros(run_sum.shape, F32)
-    run_out[...] = jnp.zeros(run_out.shape, F32)
     load.wait()
     first_half = lax.broadcasted_iota(jnp.int32, (tok, 2 * dim), 1) < dim
 
@@ -340,6 +338,10 @@
         return 0
 
     def queries():
+        run_max[...] = jnp.full(run_max.shape, -1e30, F32)
+        run_sum[...] = jnp.zeros(run_sum.shape, F32)
+        run_out[...] = jnp.zeros(run_out.shape, F32)
+        meanwhile()
         qt = nt(proj[0], normed(x[...])).astype(BF16).astype(F32) * (LOG2E * dim ** -0.5)
         hi = qt.astype(BF16)
         rest = qt - hi.astype(F32)
@@ -353,6 +355,8 @@
             qm[h, 3 * dim:4 * dim, :] = jnp.zeros((dim, tok), BF16)
 
     n_blk = 2 * tok // KEY_BLK
+    n_slot = sbuf.shape[0]
+    assert HEADS_PER_STEP * n_blk % n_slot == 0
 
     def attend(k):
         keys_over(k).wait_recv()
@@ -366,20 +370,19 @@
 
         tiles = [slice(q, q + QUERY_TILE) for q in range(0, tok, QUERY_TILE)]
 
-        def pair(p, tops):
-            for u in range(2 * n_blk):
-                h, j = 2 * p + u // n_blk, u % n_blk
-                if u + 1 < 2 * n_blk:
-                    nh, nj = 2 * p + (u + 1) // n_blk, (u + 1) % n_blk
-                else:
-                    nh, nj = jnp.minimum(2 * p + 2, n_head - 1), 0
+        def heads(p, tops):
+            for u in range(HEADS_PER_STEP * n_blk):
+                h, j = HEADS_PER_STEP * p + u // n_blk, u % n_blk
+                nh, nj = HEADS_PER_STEP * p + (u + 1) // n_blk, (u + 1) % n_blk
+                if u + 1 == HEADS_PER_STEP * n_blk:
+                    nh = jnp.minimum(nh, n_head - 1)
                 ahead = []
                 for q, cols in enumerate(tiles):
-                    ahead.append(produce(nh, nj, (u + 1) % 2, cols))
+                    ahead.append(produce(nh, nj, (u + 1) % n_slot, cols))
                     m, l, acc = run_max[h, 0:1, cols], run_sum[h, :, cols], run_out[h, :, cols]
                     new = jnp.maximum(m, jnp.max(tops[q], axis=0, keepdims=True))
                     alpha = jnp.exp2(m - new)
-                    w = jnp.exp2(sbuf[u % 2, :, cols] - new)
+                    w = jnp.exp2(sbuf[u % n_slot, :, cols] - new)
                     run_sum[h, :, cols] = l * alpha + jnp.sum(w.reshape(KEY_BLK // 8, 8, QUERY_TILE), axis=0)
                     run_max[h, 0:1, cols] = new
                     vt = vbuf[k, pl.ds(pl.multiple_of(h * dim, dim), dim), j * KEY_BLK:(j + 1) * KEY_BLK]
@@ -387,7 +390,7 @@
                 tops = ahead
             return tuple(tops)
 
-        lax.fori_loop(0, n_head // 2, pair, tuple(produce(0, 0, 0, cols) for cols in tiles))
+        lax.fori_loop(0, n_head // HEADS_PER_STEP, heads, tuple(produce(0, 0, 0, cols) for cols in tiles))
 
     def step(i, _):
         @pl.when(i > 0)
@@ -454,20 +457,24 @@
 
         stats = lax.fori_loop(0, at.seg, second, zero_stats(chan))
         loads[3].start()
-        swap_all(at, stats, mine.at[2], every.at[2], gather, ssem.at[2], rsem.at[2])
+        links = gather_links(at, xall, asend, arecv)
+        swap_all(at, stats, mine.at[2], every.at[2], gather, ssem.at[2], rsem.at[2], behind=(links[0], links[2], links[1], links[3]))
 
     pl.run_scoped(first_block, tap_shape)
+
+    def next_time():
+        temb_loads[1].wait()
+        time_terms(t_emb, tbuf, temb)
+
     dim = chan // n_head
     pl.run_scoped(
-        functools.partial(attention, at, count, every.at[2], a_norms, spread, proj, proj_load, ot, xall, kbuf, vbuf, asend, arecv),
+        functools.partial(attention, at, count, every.at[2], a_norms, spread, proj, proj_load, next_time, ot, xall, kbuf, vbuf, asend, arecv),
         pltpu.VMEM((n_head, 4 * dim, tok), BF16),
-        pltpu.VMEM((2, KEY_BLK, tok), F32),
+        pltpu.VMEM((3, KEY_BLK, tok), F32),
         pltpu.VMEM((n_head, 8, tok), F32),
         pltpu.VMEM((n_head, 8, tok), F32),
         pltpu.VMEM((n_head, dim, tok), F32),
     )
-    temb_loads[1].wait()
-    time_terms(t_emb, tbuf, temb)
     pl.run_scoped(functools.partial(second_block, at, count, norms, gather, spread, y_out, xin, hid, wbuf, mine, every, hrow, colbuf, hcol, colact, temb, proj, ot, xall, loads, ssem, rsem, ys, yr, lsem), tap_shape)
 
 

time: 161 us -> 157 us (0.975)
  Pallas kernels: 158 us -> 154 us
    pallas_call x1, Pallas kernels: 158 us -> 154 us  [run_stage(): pl.pallas_call(functools.partial(stage, dims, count, n_head), out_shape=j...]
where the time goes in v4:
time: 157 us
  Pallas kernels  154 us (98%)
  local copies, waits for them, and re-layouts  2.23 us (1%)
    pallas_call x1, Pallas kernels, run_stage(): pl.pallas_call(functools.partial(stage, dims, count, n_head), out_shape=j...  154 us

profile of v4, /device:TPU:97, one launch (start us, length us, event | category | flops | bytes accessed | tf_op | source)
XLA Modules:
  0.0 156.6 jit_solution(9404727667163010967)
XLA Ops:
  0.0 154.4 %unet_stage.1 = bf16[4,2,96,640]{3,2,1,0:T(8,128)(2,1)} custom-call(bf16[4,2,96,640]{3,2,1,0:T(8,128)(2,1)} %latent.1, bf16[4,1280]{1,0:T(4,128)(2,1)} %t_emb.1, bf16[2,1280,640]{2,1,0:T(8,128)(2,1)} %w_temb.1, bf16[2,2,2,640]{3,2,1,0:T(2,128)(2,1)} %norms.1, bf16[2,2,3,3,640,640]{5,4,3,2,1,0:T(8,128)(2,1)} %w_all.1, bf16[2,640]{1,0:T(2,128)(2,1)} %a_norms.1, ...), custom_call_target="tpu_custom_call" | custom-call | tf_op jit(solution)/shard_map/unet_stage/pallas_call | solution.py:560
  154.4 2.2 %copy.11 = bf16[4,2,96,640]{3,2,1,0:T(8,128)(2,1)} copy(bf16[4,2,96,640]{3,2,1,0:T(8,128)(2,1)} %unet_stage.1) | data formatting | bytes 1966080

commit v5 on v4

--- a/solution.py
+++ b/solution.py
@@ -244,7 +244,7 @@
     terms = norm_terms(every.at[stage], spread, *norm_rows(norms.at[blk, 0]), count)
     fill_taps(at, xin, hrow.at[halo], hcol.at[halo], terms, taps, colact)
     loads[0].wait()
-    shift = temb[pl.ds(at.img, 1), :]
+    shift = temb[blk, pl.ds(at.img, 1), :]
 
     def first(m, stats):
         h = (conv_rows(at, taps, wbuf.at[0], m * rows) + shift).astype(BF16)
@@ -281,7 +281,7 @@
     return [remote(src, dst, ssem.at[k], rsem.at[k], device) for k, (src, dst, device) in enumerate(ends)]
 
 
-def attention(at, count, every, norms, spread, proj, load, meanwhile, out, xall, kbuf, vbuf, ssem, rsem, qm, sbuf, run_max, run_sum, run_out):
+def attention(at, count, every, norms, spread, proj, load, out, xall, kbuf, vbuf, ssem, rsem, qm, sbuf, run_max, run_sum, run_out):
     _, tok, chan = xall.shape
     n_head = qm.shape[0]
     dim = chan // n_head
@@ -332,8 +332,8 @@
             swapped = pltpu.roll(both, dim, 1)
             kbuf[k, 0:tok, 4 * p * dim:(4 * p + 2) * dim] = jnp.where(first_half, both, swapped).astype(BF16)
             kbuf[k, 0:tok, (4 * p + 2) * dim:(4 * p + 4) * dim] = jnp.where(first_half, swapped, both).astype(BF16)
+        vbuf[k, :, 0:tok] = nt(proj[2], g).astype(BF16)
         keys_over(k).start()
-        vbuf[k, :, 0:tok] = nt(proj[2], g).astype(BF16)
         values_over(k).start()
         return 0
 
@@ -341,7 +341,6 @@
         run_max[...] = jnp.full(run_max.shape, -1e30, F32)
         run_sum[...] = jnp.zeros(run_sum.shape, F32)
         run_out[...] = jnp.zeros(run_out.shape, F32)
-        meanwhile()
         qt = nt(proj[0], normed(x[...])).astype(BF16).astype(F32) * (LOG2E * dim ** -0.5)
         hi = qt.astype(BF16)
         rest = qt - hi.astype(F32)
@@ -358,7 +357,7 @@
     n_slot = sbuf.shape[0]
     assert HEADS_PER_STEP * n_blk % n_slot == 0
 
-    def attend(k):
+    def attend(k, _):
         keys_over(k).wait_recv()
         values_over(k).wait_recv()
 
@@ -388,26 +387,19 @@
                     vt = vbuf[k, pl.ds(pl.multiple_of(h * dim, dim), dim), j * KEY_BLK:(j + 1) * KEY_BLK]
                     run_out[h, :, cols] = acc * alpha + jnp.dot(vt, w.astype(BF16), preferred_element_type=F32)
                 tops = ahead
+
+            @pl.when(jnp.logical_and(p == 0, k < 3))
+            def _():
+                project(k + 1, 0)
+
             return tuple(tops)
 
         lax.fori_loop(0, n_head // HEADS_PER_STEP, heads, tuple(produce(0, 0, 0, cols) for cols in tiles))
-
-    def step(i, _):
-        @pl.when(i > 0)
-        def _():
-            attend(i - 1)
-
-        start = jnp.minimum(i + i // 2, 4)
-        stop = jnp.minimum((i + 1) + (i + 1) // 2, 4)
-        lax.fori_loop(start, stop, project, 0)
-
-        @pl.when(i == 0)
-        def _():
-            queries()
-
         return 0
 
-    lax.fori_loop(0, 5, step, 0)
+    project(0, 0)
+    queries()
+    lax.fori_loop(0, 4, attend, 0)
     for copy in (low_right, high_right, high_left, low_left, far_low, far_high):
         copy.wait_send()
     for k in range(4):
@@ -422,31 +414,43 @@
     lax.fori_loop(0, n_head, finish, 0)
 
 
-def stage(dims, count, n_head, latent, t_emb, w_temb, norms, w_all, a_norms, proj_all, gather, spread, y_out, xin, hid, wbuf, mine, every, hrow, colbuf, hcol, colact, temb, tbuf, proj, ot, xall, kbuf, vbuf, wsem, ssem, rsem, xs, xr, ys, yr, lsem, asend, arecv):
+def stage(dims, count, n_head, latent, t_emb_in, w_temb, norms_in, w_all, a_norms_in, proj_all, gather_in, spread_in, y_out, t_emb, norms, a_norms, gather, spread, xin, wbuf, mine, every, hrow, colbuf, hcol, colact, temb, proj, xall, kbuf, vbuf, wsem, ssem, rsem, xs, xr, ys, yr, lsem, asend, arecv):
     at = Place(dims)
     n_wait = signal_peers(at, True)
     rows, cols, chan = at.rows, at.cols, at.chan
     tile = rows * cols
     tok = tile * at.seg
+    ot = vbuf.at[0, :, pl.ds(0, tok)]
     loads = [pltpu.make_async_copy(w_all.at[blk, j], wbuf.at[j], wsem.at[2 * blk + j]) for blk in range(2) for j in range(2)]
-    temb_loads = [pltpu.make_async_copy(w_temb.at[blk], tbuf, wsem.at[4 + blk]) for blk in range(2)]
     proj_load = pltpu.make_async_copy(proj_all, proj, wsem.at[6])
+    small = ((t_emb_in, t_emb), (norms_in, norms), (a_norms_in, a_norms), (gather_in, gather), (spread_in, spread))
+    small_loads = [pltpu.make_async_copy(src, dst, wsem.at[7 + i]) for i, (src, dst) in enumerate(small)]
+    for load in small_loads:
+        load.start()
     wait_peers(n_wait)
     images = spread_images(at, latent, xin, xs, xr, lsem, colbuf.at[0])
     next(images)
-    temb_loads[0].start()
     loads[0].start()
     loads[1].start()
     proj_load.start()
-    temb_loads[0].wait()
-    time_terms(t_emb, tbuf, temb)
-    temb_loads[1].start()
+    for load in small_loads:
+        load.wait()
+
+    def times(tbuf):
+        copies = [pltpu.make_async_copy(w_temb.at[blk], tbuf.at[blk], wsem.at[4 + blk]) for blk in range(2)]
+        for copy in copies:
+            copy.start()
+        for blk, copy in enumerate(copies):
+            copy.wait()
+            time_terms(t_emb, tbuf.at[blk], temb.at[blk])
+
+    pl.run_scoped(times, pltpu.VMEM(w_temb.shape, BF16))
     stats = next(images)
     swap_all(at, stats, mine.at[0], every.at[0], gather, ssem.at[0], rsem.at[0], xin, hrow.at[0], colbuf.at[0], hcol.at[0])
     next(images)
-    tap_shape = pltpu.VMEM((rows * at.seg + 2, cols, 3 * chan), BF16)
-
-    def first_block(taps):
+    conv_bufs = pltpu.VMEM((rows * at.seg + 2, cols, 3 * chan), BF16), pltpu.VMEM(xin.shape, BF16)
+
+    def first_block(taps, hid):
         conv_pair(at, count, 0, 0, 0, temb, norms, gather, spread, xin, hid, taps, wbuf, mine, every, hrow, colbuf, hcol, colact, loads[0:2], loads[2], ssem, rsem)
 
         def second(m, stats):
@@ -460,25 +464,21 @@
         links = gather_links(at, xall, asend, arecv)
         swap_all(at, stats, mine.at[2], every.at[2], gather, ssem.at[2], rsem.at[2], behind=(links[0], links[2], links[1], links[3]))
 
-    pl.run_scoped(first_block, tap_shape)
-
-    def next_time():
-        temb_loads[1].wait()
-        time_terms(t_emb, tbuf, temb)
+    pl.run_scoped(first_block, *conv_bufs)
 
     dim = chan // n_head
     pl.run_scoped(
-        functools.partial(attention, at, count, every.at[2], a_norms, spread, proj, proj_load, next_time, ot, xall, kbuf, vbuf, asend, arecv),
+        functools.partial(attention, at, count, every.at[2], a_norms, spread, proj, proj_load, ot, xall, kbuf, vbuf, asend, arecv),
         pltpu.VMEM((n_head, 4 * dim, tok), BF16),
         pltpu.VMEM((3, KEY_BLK, tok), F32),
         pltpu.VMEM((n_head, 8, tok), F32),
         pltpu.VMEM((n_head, 8, tok), F32),
         pltpu.VMEM((n_head, dim, tok), F32),
     )
-    pl.run_scoped(functools.partial(second_block, at, count, norms, gather, spread, y_out, xin, hid, wbuf, mine, every, hrow, colbuf, hcol, colact, temb, proj, ot, xall, loads, ssem, rsem, ys, yr, lsem), tap_shape)
-
-
-def second_block(at, count, norms, gather, spread, y_out, xin, hid, wbuf, mine, every, hrow, colbuf, hcol, colact, temb, proj, ot, xall, loads, ssem, rsem, xs, xr, lsem, taps):
+    pl.run_scoped(functools.partial(second_block, at, count, norms, gather, spread, y_out, xin, wbuf, mine, every, hrow, colbuf, hcol, colact, temb, proj, ot, xall, loads, ssem, rsem, ys, yr, lsem), *conv_bufs)
+
+
+def second_block(at, count, norms, gather, spread, y_out, xin, wbuf, mine, every, hrow, colbuf, hcol, colact, temb, proj, ot, xall, loads, ssem, rsem, xs, xr, lsem, taps, hid):
     rows, cols, chan = at.rows, at.cols, at.chan
     tile = rows * cols
     add = lax.dot_general(ot[...], proj[3], (((0,), (0,)), ((), ())), preferred_element_type=F32)
@@ -556,14 +556,18 @@
         proj = attn_proj.transpose(0, 1, 3, 2).reshape(4, n_head * dim, chan)
         n_msg = n_peer - 1 + 5
         n_stage = 5
-        vmem, anywhere = pl.BlockSpec(memory_space=pltpu.VMEM), pl.BlockSpec(memory_space=pl.ANY)
+        anywhere = pl.BlockSpec(memory_space=pl.ANY)
         return pl.pallas_call(
             functools.partial(stage, dims, count, n_head),
             out_shape=jax.ShapeDtypeStruct(latent.shape, BF16),
-            in_specs=[anywhere, vmem, anywhere, vmem, anywhere, vmem, anywhere, vmem, vmem],
+            in_specs=[anywhere] * 9,
             out_specs=anywhere,
             scratch_shapes=[
-                pltpu.VMEM((own, cols, chan), BF16),
+                pltpu.VMEM(t_emb.shape, BF16),
+                pltpu.VMEM(res_norm.shape, BF16),
+                pltpu.VMEM(attn_norm.shape, BF16),
+                pltpu.VMEM((chan, 128), BF16),
+                pltpu.VMEM((128, chan), BF16),
                 pltpu.VMEM((own, cols, chan), BF16),
                 pltpu.VMEM((2, 3, 3, chan, chan), BF16),
                 pltpu.VMEM((n_stage, 8, 128), F32),
@@ -572,14 +576,12 @@
                 pltpu.VMEM((4, 2, own, chan), F32),
                 pltpu.VMEM((4, 4, own, chan), F32),
                 pltpu.VMEM((4, own, chan), F32),
-                pltpu.VMEM((n_img, chan), F32),
-                pltpu.VMEM(res_temb.shape[1:], BF16),
+                pltpu.VMEM((2, n_img, chan), F32),
                 pltpu.VMEM((4, n_head * dim, chan), BF16),
-                pltpu.VMEM((n_head * dim, tok), BF16),
                 pltpu.VMEM((4, tok, chan), BF16),
                 pltpu.VMEM((4, 2 * tok, 2 * chan), BF16),
                 pltpu.VMEM((4, chan, 2 * tok), BF16),
-                pltpu.SemaphoreType.DMA((7,)),
+                pltpu.SemaphoreType.DMA((12,)),
                 pltpu.SemaphoreType.DMA((n_stage, n_msg)),
                 pltpu.SemaphoreType.DMA((n_stage, n_msg)),
                 pltpu.SemaphoreType.DMA((n_img,)),

time: 157 us -> 152 us (0.968)
  Pallas kernels: 154 us -> 150 us
    pallas_call x1, Pallas kernels: 154 us -> 150 us  [run_stage(): pl.pallas_call(functools.partial(stage, dims, count, n_head), out_shape=j...]
where the time goes in v5:
time: 152 us
  Pallas kernels  150 us (99%)
  local copies, waits for them, and re-layouts  2.23 us (1%)
    pallas_call x1, Pallas kernels, run_stage(): pl.pallas_call(functools.partial(stage, dims, count, n_head), out_shape=j...  150 us

profile of v5, /device:TPU:97, one launch (start us, length us, event | category | flops | bytes accessed | tf_op | source)
XLA Modules:
  0.0 151.9 jit_solution(3326097446626378521)
XLA Ops:
  0.0 149.7 %unet_stage.1 = bf16[4,2,96,640]{3,2,1,0:T(8,128)(2,1)} custom-call(bf16[4,2,96,640]{3,2,1,0:T(8,128)(2,1)} %latent.1, bf16[4,1280]{1,0:T(4,128)(2,1)} %t_emb_in.1, bf16[2,1280,640]{2,1,0:T(8,128)(2,1)} %w_temb.1, bf16[2,2,2,640]{3,2,1,0:T(2,128)(2,1)} %norms_in.1, bf16[2,2,3,3,640,640]{5,4,3,2,1,0:T(8,128)(2,1)} %w_all.1, bf16[2,640]{1,0:T(2,128)(2,1)} %a_norms_in.1, ...), custom_call_target="tpu_custom_call" | custom-call | tf_op jit(solution)/shard_map/unet_stage/pallas_call | solution.py:560
  149.7 2.2 %copy.11 = bf16[4,2,96,640]{3,2,1,0:T(8,128)(2,1)} copy(bf16[4,2,96,640]{3,2,1,0:T(8,128)(2,1)} %unet_stage.1) | data formatting | bytes 1966080
